TPU v7x, 8 devices: a whole 2x2x1 slice. The times are simulated.
8 devices in a mesh: batch: 1 (over z), tp: 2 (over y), sp: 4 (over x, core).
Axes of the slice: x: 2, y: 2, z: 1, core: 2. Of those that a mesh axis runs over, the one named last changes fastest.
Arguments:
- tokens: bfloat16 [8192, 1024], P(('batch', 'sp'))
- glob_pos: int32 [512], P('batch')
- rel_bias: float32 [16, 513], P('tp')
- w_query: bfloat16 [1024, 1024], P(None, 'tp')
- w_key: bfloat16 [1024, 1024], P(None, 'tp')
- w_value: bfloat16 [1024, 1024], P(None, 'tp')
- w_query_glob: bfloat16 [1024, 1024], P(None, 'tp')
- w_out: bfloat16 [1024, 1024], P('tp')
- w_up: bfloat16 [1024, 4096], P(None, 'tp')
- w_down: bfloat16 [4096, 1024], P('tp')
Outputs:
- output: bfloat16 [8192, 1024], P(('batch', 'sp'))
All inputs are finite; a program needn't handle non-finite values.
Results may differ from a plain program's by a relative error of at most 0.0116037.
Values are sent between devices in bfloat16 or wider.
A program may use at most 1 GiB of HBM per device.

v0:
```python
import jax
import jax.numpy as jnp
from jax import lax
from jax.sharding import PartitionSpec as P


def solution(mesh):
    n_seq = mesh.shape["sp"]
    to_right = [(sender, sender + 1) for sender in range(n_seq - 1)]
    to_left = [(sender + 1, sender) for sender in range(n_seq - 1)]

    def local_layer(tokens, glob_pos, rel_bias, w_query, w_key, w_value, w_query_glob, w_out, w_up, w_down):
        local_rows = tokens.shape[0]
        local_heads = rel_bias.shape[0]
        window = (rel_bias.shape[1] - 1) // 2
        local_dim = w_query.shape[1]
        head_dim = local_dim // local_heads
        num_glob = glob_pos.shape[0]
        n_blocks = local_rows // window
        seq_len = local_rows * n_seq
        score_scale = head_dim ** -0.5
        row_start = lax.axis_index("sp") * local_rows
        heads_shape = (local_rows, local_heads, head_dim)
        glob_shape = (num_glob, local_heads, head_dim)

        def project(weight):
            return jnp.dot(tokens, weight, preferred_element_type=jnp.float32).astype(jnp.bfloat16)

        q_flat = project(w_query)
        k_flat = project(w_key)
        v_flat = project(w_value)
        local_slot = glob_pos - row_start
        is_owned = (local_slot >= 0) & (local_slot < local_rows)
        safe_slot = jnp.clip(local_slot, 0, local_rows - 1)
        zero_half = jnp.zeros((), jnp.bfloat16)

        def pick_rows(source):
            return jnp.where(is_owned[:, None], jnp.take(source, safe_slot, axis=0), zero_half)

        qg_part = jnp.dot(pick_rows(tokens), w_query_glob, preferred_element_type=jnp.float32).astype(jnp.bfloat16)
        glob_rows = lax.psum(jnp.stack([qg_part, pick_rows(k_flat), pick_rows(v_flat)]), "sp")
        glob_q = glob_rows[0].reshape(glob_shape)
        glob_k = glob_rows[1].reshape(glob_shape)
        glob_v = glob_rows[2].reshape(glob_shape)

        kv_loc = jnp.stack([k_flat, v_flat]).reshape((2,) + heads_shape)
        left_halo = lax.ppermute(kv_loc[:, local_rows - window:], "sp", to_right)
        right_halo = lax.ppermute(kv_loc[:, :window], "sp", to_left)
        kv_ext = jnp.concatenate([left_halo, kv_loc, right_halo], axis=1)
        kv_blocks = kv_ext.reshape(2, n_blocks + 2, window, local_heads, head_dim)
        kv_win = jnp.concatenate([kv_blocks[:, :-2], kv_blocks[:, 1:-1], kv_blocks[:, 2:]], axis=2)
        q_blocks = q_flat.reshape(n_blocks, window, local_heads, head_dim)

        rel_offs = jnp.arange(3 * window)[None, :] - jnp.arange(window)[:, None]
        in_band = (rel_offs >= 0) & (rel_offs <= 2 * window)
        band_bias = jnp.take(rel_bias, jnp.clip(rel_offs, 0, 2 * window), axis=1)
        blk_start = row_start + jnp.arange(n_blocks) * window
        key_pos = blk_start[:, None] - window + jnp.arange(3 * window)[None, :]
        key_ok = (key_pos >= 0) & (key_pos < seq_len)
        win_mask = in_band[None, None] & key_ok[:, None, None, :]
        win_scores = jnp.einsum("cqhd,ckhd->chqk", q_blocks, kv_win[0], preferred_element_type=jnp.float32)
        win_scores = jnp.where(win_mask, win_scores * score_scale + band_bias, -jnp.inf)
        query_pos = blk_start[:, None] + jnp.arange(window)[None, :]
        far_mask = jnp.abs(query_pos[:, :, None] - glob_pos[None, None, :]) > window
        glob_scores = jnp.einsum("cqhd,ghd->chqg", q_blocks, glob_k, preferred_element_type=jnp.float32)
        glob_scores = jnp.where(far_mask[:, None], glob_scores * score_scale, -jnp.inf)
        row_max = jnp.maximum(win_scores.max(axis=-1), glob_scores.max(axis=-1))[..., None]
        win_exp = jnp.exp(win_scores - row_max)
        glob_exp = jnp.exp(glob_scores - row_max)
        soft_sum = win_exp.sum(axis=-1, keepdims=True) + glob_exp.sum(axis=-1, keepdims=True)
        win_out = jnp.einsum("chqk,ckhd->cqhd", (win_exp / soft_sum).astype(jnp.bfloat16), kv_win[1], preferred_element_type=jnp.float32)
        win_out = win_out + jnp.einsum("chqg,ghd->cqhd", (glob_exp / soft_sum).astype(jnp.bfloat16), glob_v, preferred_element_type=jnp.float32)
        win_out = win_out.astype(jnp.bfloat16).reshape(heads_shape)

        part_scores = jnp.einsum("ghd,rhd->hgr", glob_q, kv_loc[0], preferred_element_type=jnp.float32) * score_scale
        part_max = part_scores.max(axis=-1)
        part_exp = jnp.exp(part_scores - part_max[..., None])
        part_sum = part_exp.sum(axis=-1)
        part_out = jnp.einsum("hgr,rhd->ghd", part_exp.astype(jnp.bfloat16), kv_loc[1], preferred_element_type=jnp.float32)
        glob_max = lax.pmax(part_max, "sp")
        rescale = jnp.exp(part_max - glob_max)
        tot_sum, tot_out = lax.psum((part_sum * rescale, part_out * rescale.T[:, :, None]), "sp")
        glob_out = (tot_out / tot_sum.T[:, :, None]).astype(jnp.bfloat16)
        slot_rows = jnp.where(is_owned, local_slot, local_rows)
        heads_out = win_out.at[slot_rows].set(glob_out, mode="drop")

        attn_part = jnp.dot(heads_out.reshape(local_rows, local_dim), w_out, preferred_element_type=jnp.float32)
        attn_proj = lax.psum(attn_part, "tp")
        hidden = (tokens.astype(jnp.float32) + attn_proj).astype(jnp.bfloat16)
        act_vals = jax.nn.gelu(jnp.dot(hidden, w_up, preferred_element_type=jnp.float32)).astype(jnp.bfloat16)
        mlp_out = lax.psum(jnp.dot(act_vals, w_down, preferred_element_type=jnp.float32), "tp")
        return (hidden.astype(jnp.float32) + mlp_out).astype(jnp.bfloat16)

    row_spec = P(("batch", "sp"), None)
    col_spec = P(None, "tp")
    head_spec = P("tp", None)
    in_specs = (row_spec, P("batch"), head_spec, col_spec, col_spec, col_spec, col_spec, head_spec, col_spec, head_spec)
    return jax.shard_map(local_layer, mesh=mesh, in_specs=in_specs, out_specs=row_spec, check_vma=False)
```

profile of v0, /device:TPU:0, one launch (start us, length us, event | category | flops | bytes accessed | tf_op | source)
XLA Modules:
  0.0 1571.2 jit_solution(10824384638079820466)
XLA Ops:
  14.2 6.2 gather_fusion.1
  24.9 6.2 convolution_convert_fusion.1
  58.1 6.1 convolution_convert_fusion
  76.2 712.1 %gather_fusion = f32[196608,8]{1,0:T(8,128)} fusion(f32[8,513]{0,1:T(8,128)S(1)} %copy.71, s32[196608]{0:T(1024)} %broadcast_clamp_fusion), kind=kCustom, calls=%fused_computation.2 | custom fusion | bytes 13369344 | tf_op jit(solution)/shard_map/jit(_take)/gather | solution.py:56
  788.4 55.5 %copy.72 = f32[256,768,8]{1,0,2:T(8,128)} copy(f32[256,768,8]{2,1,0:T(8,128)} %bitcast.4) | data formatting | bytes 12582912 | tf_op jit(solution)/shard_map/jit(_take)/gather | solution.py:56
  845.8 6.1 select_bitcast_fusion
  857.1 11.2 reshape.167
  868.4 8.3 fusion.62
  884.2 25.2 %fusion.1 = (f32[8,8,256]{2,1,0:T(8,128)S(1)}, f32[8,8,256,768]{3,2,1,0:T(8,128)}) fusion(f32[8,256,768]{2,1,0:T(8,128)S(1)} %bitcast.86, pred[8,256,768]{2,1,0:T(8,128)(4,1)} %broadcast_and_fusion, bf16[2,8,768,8,64]{2,4,3,1,0:T(8,128)(2,1)} %copy-done.7, bf16[8,256,8,64]{1,0,3,2:T(8,128)(2,1)} %bitcast.93), kind=kOutput, calls=%fused_computation.13 | convolution fusion | flops 1660928000 | bytes 66650112 | tf_op jit(solution)/shard_map/cqhd,ckhd->chqk/dot_general | solution.py:61
  912.9 15.8 %fusion.5 = (f32[8,8,256]{2,0,1:T(8,128)S(1)}, f32[8,512,8,256]{3,1,2,0:T(8,128)}) fusion(pred[8,256,512]{1,2,0:T(8,128)(4,1)} %abs_compare_fusion, bf16[512,8,64,1]{0,2,3,1:T(8,128)(2,1)S(1)} %bitcast.98, bf16[8,256,8,64]{1,0,3,2:T(8,128)(2,1)} %bitcast.94), kind=kOutput, calls=%fused_computation.18 | convolution fusion | flops 1098891264 | bytes 37289984 | tf_op jit(solution)/shard_map/cqhd,ghd->chqg/dot_general | solution.py:65
  928.8 22.5 %fusion = f32[8,8,256]{2,1,0:T(8,128)S(1)} fusion(f32[8,8,256,768]{3,2,1,0:T(8,128)} %get-tuple-element.22, f32[8,8,256]{2,1,0:T(8,128)S(1)} %copy_maximum_fusion, f32[8,256,768]{2,1,0:T(8,128)} %select_bitcast_fusion, pred[8,256,768]{2,1,0:T(8,128)(4,1)S(1)} %copy-done.5), kind=kLoop, calls=%fused_computation.8 | loop fusion | flops 62898176 | bytes 58327040 | tf_op jit(solution)/shard_map/reduce_sum | solution.py:70
  951.3 14.4 fusion.2
  967.8 14.3 multiply_reduce_fusion
  982.1 11.9 pmax.7
  994.0 14.2 fusion.3
  1008.2 14.6 fusion.31
  1022.9 17.6 %fusion.15 = f32[8,64,8,256]{3,1,0,2:T(8,128)} fusion(bf16[512,8,64,1]{0,2,1,3:T(8,128)(2,1)} %bitcast.100, f32[8,512,8,256]{3,1,2,0:T(8,128)} %get-tuple-element.24, f32[8,8,256]{2,0,1:T(8,128)S(1)} %copy.81, f32[8,8,256]{2,0,1:T(8,128)S(1)} %copy.78, pred[8,256,512]{1,2,0:T(8,128)(4,1)} %abs_compare_fusion), kind=kOutput, calls=%fused_computation.29 | convolution fusion | flops 1115684864 | bytes 39452672 | tf_op jit(solution)/shard_map/chqg,ghd->cqhd/dot_general | solution.py:72
  1040.5 27.9 %fusion.24 = bf16[8,256,8,64]{1,3,2,0:T(8,128)(2,1)S(1)} fusion(f32[8,64,8,256]{3,1,0,2:T(8,128)} %fusion.15, f32[8,8,256,768]{3,2,1,0:T(8,128)} %get-tuple-element.22, f32[8,8,256]{2,1,0:T(8,128)S(1)} %copy_add_fusion, f32[8,8,256]{2,1,0:T(8,128)S(1)} %copy_maximum_fusion, f32[8,256,768]{2,1,0:T(8,128)} %select_bitcast_fusion, ...), kind=kOutput, calls=%fused_computation.45 | convolution fusion | flops 1688207360 | bytes 70909952 | tf_op jit(solution)/shard_map/chqk,ckhd->cqhd/dot_general | solution.py:71
  1072.0 10.1 psum.37
  1084.2 46.6 %scatter_fusion = bf16[2048,8,64]{2,1,0:T(8,128)(2,1)} fusion(bf16[2048,8,64]{2,1,0:T(8,128)(2,1)} %bitcast.95, s32[512]{0:T(512)S(1)} %copy-done.11, bf16[512,8,64]{2,1,0:T(8,128)(2,1)S(1)} %copy.86), kind=kCustom, calls=%fused_computation.4 | custom fusion | bytes 1574912 | tf_op jit(solution)/shard_map/scatter | solution.py:85
  1141.0 193.9 %all-reduce.9.cloned.1.call-done = f32[2048,1024]{1,0:T(8,128)} async-done(((f32[2048,1024]{1,0:T(8,128)}), f32[2048,1024]{1,0:T(8,128)}) %all-reduce.9.cloned.1.call-update) | async-done | bytes 8388624 | tf_op jit(solution)/shard_map/psum | solution.py:88
  1334.9 25.3 %fusion.19 = f32[2048,1024]{1,0:T(8,128)} fusion(bf16[2048,1024]{1,0:T(8,128)(2,1)} %param.21, bf16[1024,2048]{1,0:T(8,128)(2,1)} %param.20, f32[2048,1024]{1,0:T(8,128)} %all-reduce.9.cloned.1.call-done, bf16[2048,1024]{1,0:T(8,128)(2,1)} %param.12), kind=kOutput, calls=%fused_computation.34 | convolution fusion | flops 17223909376 | bytes 29360128 | tf_op jit(solution)/shard_map/dot_general | solution.py:91
  1360.3 192.7 %all-reduce.11.cloned.1.call-done = f32[2048,1024]{1,0:T(8,128)} async-done(((f32[2048,1024]{1,0:T(8,128)}), f32[2048,1024]{1,0:T(8,128)}) %all-reduce.11.cloned.1.call-update) | async-done | bytes 8388624 | tf_op jit(solution)/shard_map/psum | solution.py:91
  1552.9 11.5 add_convert_fusion
  (86 shorter events, 87.3 us)
Async XLA Ops:
  6.5 1128.8 %copy-start = (bf16[512,1024]{1,0:T(8,128)(2,1)S(1)}, bf16[512,1024]{1,0:T(8,128)(2,1)}, u32[]{:S(2)}) copy-start(bf16[512,1024]{1,0:T(8,128)(2,1)} %param.19) | copy-start | bytes 3145732
  6.5 902.9 %all-reduce.5.cloned.1.call-start = ((), (), s32[]{:S(2)}) async-start(), calls=%async_computation | async-start | bytes 3145728 | tf_op jit(solution)/shard_map/psum | solution.py:41
  6.5 7.6 copy-start.10
  11.5 840.4 %copy-start.1 = (bf16[2048,512]{0,1:T(8,128)(2,1)}, bf16[2048,512]{0,1:T(8,128)(2,1)S(1)}, u32[]{:S(2)}) copy-start(bf16[2048,512]{0,1:T(8,128)(2,1)S(1)} %convolution_convert_fusion.2) | copy-start | bytes 6291460
  44.6 1037.4 %all-reduce.7.cloned.1.call-start = ((), (), s32[]{:S(2)}) async-start(), calls=%async_computation.1 | async-start | bytes 2097152 | tf_op jit(solution)/shard_map/psum | solution.py:82
  46.8 805.1 %collective-permute-start.1 = (bf16[2,256,8,64]{1,3,2,0:T(8,128)(2,1)}, bf16[2,256,8,64]{1,3,2,0:T(8,128)(2,1)}, u32[]{:S(2)}, u32[]{:S(2)}) collective-permute-start(bf16[2,256,8,64]{1,3,2,0:T(8,128)(2,1)} %get-tuple-element.12), channel_id=1, source_target_pairs={{1,0},{2,1},{3,2},{5,4},{6,5},{7,6}} | collective-permute-start | bytes 1572872 | tf_op jit(solution)/shard_map/ppermute | solution.py:48
  48.1 803.8 %collective-permute-start = (bf16[2,256,8,64]{1,3,2,0:T(8,128)(2,1)}, bf16[2,256,8,64]{1,3,2,0:T(8,128)(2,1)}, u32[]{:S(2)}, u32[]{:S(2)}) collective-permute-start(bf16[2,256,8,64]{1,3,2,0:T(8,128)(2,1)} %get-tuple-element.11), channel_id=1, source_target_pairs={{0,1},{1,2},{2,3},{4,5},{5,6},{6,7}} | collective-permute-start | bytes 1572872 | tf_op jit(solution)/shard_map/ppermute | solution.py:47
  58.1 13.7 copy-start.9
  788.3 55.6 %copy-start.8 = (pred[256,768]{1,0:T(8,128)(4,1)S(1)}, pred[256,768]{1,0:T(8,128)(4,1)}, u32[]{:S(2)}) copy-start(pred[256,768]{1,0:T(8,128)(4,1)} %fusion.44) | copy-start | bytes 589828
  843.9 8.0 copy-start.3
  877.7 6.5 slice-start
  878.7 5.5 slice-start.1
  879.7 4.5 copy-start.7
  912.9 15.8 %copy-start.5 = (pred[8,256,768]{2,1,0:T(8,128)(4,1)S(1)}, pred[8,256,768]{2,1,0:T(8,128)(4,1)}, u32[]{:S(2)}) copy-start(pred[8,256,768]{2,1,0:T(8,128)(4,1)} %broadcast_and_fusion) | copy-start | bytes 4718596
  951.3 16.6 %copy-start.2 = (bf16[2048,512]{0,1:T(8,128)(2,1)S(1)}, bf16[2048,512]{0,1:T(8,128)(2,1)}, u32[]{:S(2)}) copy-start(bf16[2048,512]{0,1:T(8,128)(2,1)} %copy-done.1) | copy-start | bytes 6291460
  994.0 14.2 copy-start.4
  1022.8 312.1 %all-reduce.9.cloned.1.call-start = ((), (), s32[]{:S(2)}) async-start(), calls=%async_computation.2 | async-start | bytes 16777216 | tf_op jit(solution)/shard_map/psum | solution.py:88
  1022.9 17.6 %copy-start.6 = (pred[8,256,768]{2,1,0:T(8,128)(4,1)S(1)}, pred[8,256,768]{2,1,0:T(8,128)(4,1)}, u32[]{:S(2)}) copy-start(pred[8,256,768]{2,1,0:T(8,128)(4,1)} %broadcast_and_fusion) | copy-start | bytes 4718596
  1068.4 15.8 %copy-start.11 = (s32[512]{0:T(512)S(1)}, s32[512]{0:T(512)}, u32[]{:S(2)}) copy-start(s32[512]{0:T(512)} %compare_select_fusion.2) | copy-start | bytes 6148
  1140.9 412.0 %all-reduce.11.cloned.1.call-start = ((), (), s32[]{:S(2)}) async-start(), calls=%async_computation.3 | async-start | bytes 16777216 | tf_op jit(solution)/shard_map/psum | solution.py:91
Sparse Core Ops, SparseCore 0:
  44.7 45.6 all-reduce.4
  1023.0 31.7 all-reduce.6
  1141.1 193.7 all-reduce.8
  1360.4 192.5 all-reduce.10
where the time goes:
time: 1600 us; the launch traced here: 1570 us
  local copies, waits for them, and re-layouts  887 us (55%)
  waiting for transfers between devices  387 us (24%)
  matrix products  166 us (10%)
  other arithmetic  89.7 us (6%)
  blocking collectives  22 us (1%)
    gather x2, local copies, waits for them, and re-layouts, local_layer(): band_bias = jnp.take(rel_bias, jnp.clip(rel_offs, 0, 2 * window), axis=1)  768 us
    psum x1, waiting for transfers between devices, local_layer(): attn_proj = lax.psum(attn_part, 'tp')  194 us
    psum x1, waiting for transfers between devices, local_layer(): lax.psum(jnp.dot(act_vals, w_down, preferred_element_type=jnp.float32), '...  193 us
    scatter x2, local copies, waits for them, and re-layouts, local_layer(): heads_out = win_out.at[slot_rows].set(glob_out, mode='drop')  51.1 us
  transfers between devices with their start and end apart: 6, of which 2 were waited for; matrix products, arithmetic and copies ran while one was open for 57% of the time, Pallas kernels for 0%

commit v1 on v0

v1 whole, which is shorter than its diff:
```python
import functools

import jax
import jax.numpy as jnp
from jax import lax
from jax.experimental import pallas as pl
from jax.experimental.pallas import tpu as pltpu
from jax.sharding import PartitionSpec as P

BF = jnp.bfloat16
F32 = jnp.float32
NEG = float("-inf")
QB = 128


def const_spec(shape):
    return pl.BlockSpec(shape, lambda *_: (0,) * len(shape), pipeline_mode=pl.Buffered(1))


def pair_rhs(q_pair):
    half = lax.broadcasted_iota(jnp.int32, q_pair.shape, 0) < q_pair.shape[0] // 2
    zero = jnp.zeros_like(q_pair)
    return jnp.concatenate([jnp.where(half, q_pair, zero), jnp.where(half, zero, q_pair)], axis=1)


def unpair(o_two):
    n = o_two.shape[1] // 2
    half = lax.broadcasted_iota(jnp.int32, (o_two.shape[0], n), 0) < o_two.shape[0] // 2
    return jnp.where(half, o_two[:, :n], o_two[:, n:])


def window_kernel(base, n_win, info_ref, q_ref, k_ref, vt_ref, kg_ref, vgt_ref, br_ref, gpos_ref, o_ref, bias, gmask, score):
    j = pl.program_id(0)
    blk = j + base
    row_start = info_ref[0]
    seq_len = info_ref[1]
    n_pairs = q_ref.shape[0] // 128
    n_glob = kg_ref.shape[0]

    @pl.when(j == 0)
    def _():
        for head in range(2 * n_pairs):
            lanes = slice((head % 2) * QB, (head % 2 + 1) * QB)
            for c in range(n_win):
                hi = 128 * (n_win - c)
                g = jnp.concatenate([br_ref[head:head + 1, hi:hi + 128], br_ref[head:head + 1, hi - 128:hi]], axis=1)
                rolled = pltpu.roll(jnp.broadcast_to(g, (128, 256)), 0, 1, stride=1, stride_axis=0)
                bias[head // 2, c, :, lanes] = rolled[:, :QB]
            bias[head // 2, n_win, :, lanes] = jnp.full((128, QB), NEG, F32)

    q_start = row_start + blk * QB
    q_pos = q_start + lax.broadcasted_iota(jnp.int32, (n_glob, QB), 1)
    gmask[...] = jnp.where(jnp.abs(q_pos - gpos_ref[...]) > (n_win - 1) * 64, 0.0, NEG)

    slots = []
    for c in range(n_win):
        key_start = q_start - (n_win - 1) * 64 + 128 * c
        slots.append(jnp.where((key_start >= 0) & (key_start < seq_len), c, n_win))
    n_chunk = n_win + n_glob // 128
    for p in range(n_pairs):
        lanes = slice(128 * p, 128 * p + 128)
        buf = p % 2
        rhs = pair_rhs(q_ref[lanes, :])
        top = None
        for c in range(n_chunk):
            if c < n_win:
                keys = k_ref[pl.ds(pl.multiple_of(blk * QB + 128 * c, 128), 128), lanes]
                extra = bias[p, slots[c]]
            else:
                rows = slice(128 * (c - n_win), 128 * (c - n_win) + 128)
                keys = kg_ref[rows, lanes]
                extra = jnp.concatenate([gmask[rows, :], gmask[rows, :]], axis=1)
            s = jnp.dot(keys, rhs, preferred_element_type=F32) + extra
            score[buf, 128 * c:128 * c + 128, :] = s
            part = jnp.max(s.reshape(16, 8, 2 * QB), axis=0)
            top = part if top is None else jnp.maximum(top, part)
        top = jnp.max(top, axis=0, keepdims=True)
        total = None
        for c in range(n_chunk):
            rows = slice(128 * c, 128 * c + 128)
            e = jnp.exp(score[buf, rows, :] - top)
            score[buf, rows, :] = e
            part = jnp.sum(e.reshape(16, 8, 2 * QB), axis=0)
            total = part if total is None else total + part
        inv = 1.0 / jnp.sum(total, axis=0, keepdims=True)
        w_len = 128 * n_win
        pw = (score[buf, :w_len, :] * inv).astype(BF)
        pg = (score[buf, w_len:, :] * inv).astype(BF)
        vt = vt_ref[lanes, pl.ds(pl.multiple_of(blk * QB, 128), w_len)]
        o_two = jnp.dot(vt, pw, preferred_element_type=F32) + jnp.dot(vgt_ref[lanes, :], pg, preferred_element_type=F32)
        o_ref[:, lanes] = jnp.transpose(unpair(o_two)).astype(BF)


def glob_kernel(q_ref, k_ref, vt_ref, o_ref, m_ref, l_ref, score):
    rows = k_ref.shape[0]
    rhs = pair_rhs(q_ref[...])
    top = None
    for c in range(rows // 256):
        s = jnp.dot(k_ref[256 * c:256 * c + 256, :], rhs, preferred_element_type=F32)
        score[256 * c:256 * c + 256, :] = s
        part = jnp.max(s.reshape(32, 8, 2 * QB), axis=0)
        top = part if top is None else jnp.maximum(top, part)
    top = jnp.max(top, axis=0, keepdims=True)
    total = None
    acc = None
    for c in range(rows // 256):
        e = jnp.exp(score[256 * c:256 * c + 256, :] - top)
        part = jnp.sum(e.reshape(32, 8, 2 * QB), axis=0)
        total = part if total is None else total + part
        o = jnp.dot(vt_ref[:, 256 * c:256 * c + 256], e.astype(BF), preferred_element_type=F32)
        acc = o if acc is None else acc + o
    o_ref[...] = unpair(acc)
    m_ref[0] = jnp.broadcast_to(top, (8, 2 * QB))
    l_ref[0] = jnp.broadcast_to(jnp.sum(total, axis=0, keepdims=True), (8, 2 * QB))


def mlp_kernel(info_ref, x_ref, oa_ref, ob_ref, wo_ref, wu_ref, wd_ref, *refs):
    wo_p, wu_p, wd_p, out_ref = refs[0:4], refs[4:8], refs[8:12], refs[12]
    piece = wu_p[0].shape[1]
    acc = x_ref[...].astype(F32) + jnp.dot(oa_ref[...], wo_ref[...], preferred_element_type=F32)
    for k in range(4):
        depth = wo_p[k].shape[0]
        cols = pl.ds(pl.multiple_of(info_ref[2 + k] * depth, depth), depth)
        acc = acc + jnp.dot(ob_ref[:, cols], wo_p[k][...], preferred_element_type=F32)
    h = acc.astype(BF)
    acc = h.astype(F32)
    for k in range(8):
        cols = slice(piece * (k % 4), piece * (k % 4) + piece)
        up = wu_ref[:, cols] if k < 4 else wu_p[k - 4][...]
        down = wd_ref[cols, :] if k < 4 else wd_p[k - 4][...]
        act = jax.nn.gelu(jnp.dot(h, up, preferred_element_type=F32)).astype(BF)
        acc = acc + jnp.dot(act, down, preferred_element_type=F32)
    out_ref[...] = acc.astype(BF)


def solution(mesh):
    n_seq = mesh.shape["sp"]
    to_right = [(s, s + 1) for s in range(n_seq - 1)]
    to_left = [(s + 1, s) for s in range(n_seq - 1)]
    flip = {"tp": [(0, 1), (1, 0)], 1: [(s, s ^ 1) for s in range(n_seq)], 2: [(s, s ^ 2) for s in range(n_seq)]}

    def swap_tp(v):
        return lax.ppermute(v, "tp", flip["tp"])

    def swap_core(v):
        return lax.ppermute(v, "sp", flip[1])

    def swap_x(v):
        return lax.ppermute(v, "sp", flip[2])

    def local_layer(tokens, glob_pos, rel_bias, w_query, w_key, w_value, w_query_glob, w_out, w_up, w_down):
        rows, dim = tokens.shape
        heads, span = rel_bias.shape
        window = (span - 1) // 2
        loc = w_query.shape[1]
        head_dim = loc // heads
        n_glob = glob_pos.shape[0]
        n_pairs = loc // 128
        n_win = 2 * window // 128 + 1
        scale = head_dim ** -0.5
        rank = lax.axis_index("sp")
        core = rank % 2
        row_start = rank * rows
        vmem = 60 * 1024 * 1024

        def dot(a, b, dims):
            return lax.dot_general(a, b, (dims, ((), ())), preferred_element_type=F32)

        def quarters(w, axis):
            size = w.shape[axis] // n_seq
            mine = swap_tp(lax.dynamic_slice_in_dim(w, rank * size, size, axis))
            across = swap_x(mine)
            return [mine, across, swap_core(mine), swap_core(across)]

        wo_p = quarters(w_out, 0)
        wu_p = quarters(w_up, 1)
        wd_p = quarters(w_down, 0)

        slot = glob_pos - row_start
        pick = (slot[:, None] == jnp.arange(rows)[None, :]).astype(BF)
        x_glob = dot(pick, tokens, ((1,), (0,))).astype(BF)
        x_glob = x_glob + swap_core(x_glob)
        half = n_glob // 2
        x_half = lax.dynamic_slice_in_dim(x_glob, core * half, half, 0)
        x_half = x_half + swap_x(x_half)
        x_other = swap_core(x_half)
        first = core == 0
        x_glob = jnp.concatenate([jnp.where(first, x_half, x_other), jnp.where(first, x_other, x_half)], axis=0)

        q_t = dot(w_query, tokens, ((0,), (1,))).astype(BF) * BF(scale)
        k_loc = dot(tokens, w_key, ((1,), (0,))).astype(BF)
        v_t = dot(w_value, tokens, ((0,), (1,))).astype(BF)
        kg = dot(x_glob, w_key, ((1,), (0,))).astype(BF)
        vg_t = dot(w_value, x_glob, ((0,), (1,))).astype(BF)
        qg_t = dot(w_query_glob, x_glob, ((0,), (1,))).astype(BF) * BF(scale)

        k_ext = jnp.concatenate([
            lax.ppermute(k_loc[rows - window:], "sp", to_right), k_loc, lax.ppermute(k_loc[:window], "sp", to_left)], axis=0)
        v_ext = jnp.concatenate([
            lax.ppermute(v_t[:, rows - window:], "sp", to_right), v_t, lax.ppermute(v_t[:, :window], "sp", to_left)], axis=1)

        n_tiles = n_glob // QB
        part_o, part_m, part_l = pl.pallas_call(
            glob_kernel,
            name="glob_attn",
            grid=(n_pairs, n_tiles),
            in_specs=[
                pl.BlockSpec((128, QB), lambda p, t: (p, t)),
                pl.BlockSpec((rows, 128), lambda p, t: (0, p)),
                pl.BlockSpec((128, rows), lambda p, t: (p, 0)),
            ],
            out_specs=[
                pl.BlockSpec((128, QB), lambda p, t: (p, t)),
                pl.BlockSpec((1, 8, 2 * QB), lambda p, t: (p * n_tiles + t, 0, 0)),
                pl.BlockSpec((1, 8, 2 * QB), lambda p, t: (p * n_tiles + t, 0, 0)),
            ],
            out_shape=[
                jax.ShapeDtypeStruct((loc, n_glob), F32),
                jax.ShapeDtypeStruct((n_pairs * n_tiles, 8, 2 * QB), F32),
                jax.ShapeDtypeStruct((n_pairs * n_tiles, 8, 2 * QB), F32),
            ],
            scratch_shapes=[pltpu.VMEM((rows, 2 * QB), F32)],
            compiler_params=pltpu.CompilerParams(vmem_limit_bytes=vmem),
            cost_estimate=pl.CostEstimate(flops=16 * 10**9, bytes_accessed=8 * 2**20, transcendentals=heads * n_glob * rows),
        )(qg_t, k_loc, v_t)

        def stat(s):
            s = s[:, 0, :].reshape(n_pairs, n_tiles, 2, QB)
            return s.transpose(0, 2, 1, 3).reshape(heads, n_glob)

        stats = jnp.stack([stat(part_m), stat(part_l)])
        for swap in (swap_core, swap_x):
            o_far, s_far = swap(part_o), swap(stats)
            top = jnp.maximum(stats[0], s_far[0])
            mine, theirs = jnp.exp(stats[0] - top), jnp.exp(s_far[0] - top)
            stats = jnp.stack([top, stats[1] * mine + s_far[1] * theirs])
            shape = (heads, head_dim, n_glob)
            part_o = (part_o.reshape(shape) * mine[:, None] + o_far.reshape(shape) * theirs[:, None]).reshape(loc, n_glob)
        glob_o = (part_o.reshape(heads, head_dim, n_glob) / stats[1][:, None]).astype(BF).reshape(loc, n_glob)

        br = jnp.pad(rel_bias[:, ::-1], ((0, 0), (128, 127)), constant_values=NEG)
        info = jnp.stack([row_start, jnp.int32(rows * n_seq), rank, rank ^ 2, rank ^ 1, rank ^ 3]).astype(jnp.int32)
        n_ext = rows + 2 * window
        n_calls = 2
        blocks = rows // QB // n_calls
        is_glob = (slot[:, None] == jnp.arange(rows)[None, :]).any(axis=0)
        o_mine, o_peer = [], []
        for call in range(n_calls):
            base = call * blocks
            o_win = pl.pallas_call(
                functools.partial(window_kernel, base, n_win),
                name="window_attn",
                grid=(blocks,),
                in_specs=[
                    pl.BlockSpec(memory_space=pltpu.SMEM),
                    pl.BlockSpec((loc, QB), functools.partial(lambda b, j: (0, j + b), base)),
                    const_spec((n_ext, loc)),
                    const_spec((loc, n_ext)),
                    const_spec((n_glob, loc)),
                    const_spec((loc, n_glob)),
                    const_spec((heads, span + 255)),
                    const_spec((n_glob, 1)),
                ],
                out_specs=pl.BlockSpec((QB, loc), lambda j: (j, 0)),
                out_shape=jax.ShapeDtypeStruct((blocks * QB, loc), BF),
                scratch_shapes=[
                    pltpu.VMEM((n_pairs, n_win + 1, 128, 2 * QB), F32),
                    pltpu.VMEM((n_glob, QB), F32),
                    pltpu.VMEM((2, n_win * 128 + n_glob, 2 * QB), F32),
                ],
                compiler_params=pltpu.CompilerParams(vmem_limit_bytes=vmem),
                cost_estimate=pl.CostEstimate(flops=16 * 10**9, bytes_accessed=8 * 2**20, transcendentals=heads * n_glob * rows),
            )(info, q_t, k_ext, v_ext, kg, vg_t, br, glob_pos[:, None])
            part = slice(base * QB, (base + blocks) * QB)
            glob_rows = dot(pick[:, part], glob_o, ((0,), (1,))).astype(BF)
            o_fix = jnp.where(is_glob[part, None], glob_rows, o_win)
            o_mine.append(o_fix)
            o_peer.append(swap_tp(o_fix))
        oa = jnp.concatenate(o_mine, axis=0)
        ob = jnp.concatenate(o_peer, axis=0)

        mb = 256
        hid = w_up.shape[1]
        piece = hid // n_seq
        return pl.pallas_call(
            mlp_kernel,
            name="mlp",
            grid=(rows // mb,),
            in_specs=[
                pl.BlockSpec(memory_space=pltpu.SMEM),
                pl.BlockSpec((mb, dim), lambda j: (j, 0)),
                pl.BlockSpec((mb, loc), lambda j: (j, 0)),
                pl.BlockSpec((mb, loc), lambda j: (j, 0)),
                const_spec((loc, dim)),
                const_spec((dim, hid)),
                const_spec((hid, dim)),
                *[const_spec((loc // n_seq, dim))] * 4,
                *[const_spec((dim, piece))] * 4,
                *[const_spec((piece, dim))] * 4,
            ],
            out_specs=pl.BlockSpec((mb, dim), lambda j: (j, 0)),
            out_shape=jax.ShapeDtypeStruct((rows, dim), BF),
            compiler_params=pltpu.CompilerParams(vmem_limit_bytes=vmem),
            cost_estimate=pl.CostEstimate(flops=38 * 10**9, bytes_accessed=30 * 2**20, transcendentals=rows * hid * 2),
        )(info, tokens, oa, ob, w_out, w_up, w_down, *wo_p, *wu_p, *wd_p)

    row_spec = P(("batch", "sp"), None)
    col_spec = P(None, "tp")
    head_spec = P("tp", None)
    in_specs = (row_spec, P("batch"), head_spec, col_spec, col_spec, col_spec, col_spec, head_spec, col_spec, head_spec)
    return jax.shard_map(local_layer, mesh=mesh, in_specs=in_specs, out_specs=row_spec, check_vma=False)
```

time: 1600 us -> 282 us (0.18); the launches traced: 1570 us -> 281 us
  local copies, waits for them, and re-layouts: 887 us -> 16.3 us
  waiting for transfers between devices: 387 us -> 64.7 us
  matrix products: 166 us -> 24.5 us
  Pallas kernels: 0 us -> 137 us
  other arithmetic: 89.7 us -> 14.2 us
  blocking collectives: 22 us -> 0 us
  starting transfers between devices: 6.05 us -> 24.1 us
    gather x5 -> x0, local copies, waits for them, and re-layouts: 783 us -> none  [the longest x2 768 us: local_layer(): band_bias = jnp.take(rel_bias, jnp.clip(rel_offs, 0, 2 * window), axis=1)]
    psum x4 -> x0, waiting for transfers between devices: 387 us -> none  [the longest x1 194 us: local_layer(): attn_proj = lax.psum(attn_part, 'tp')]
    dot_general x12 -> x9, matrix products: 166 us -> 24.5 us  [dot(): return lax.dot_general(a, b, (dims, ((), ())), preferred_element_type=F32)]
    pallas_call x0 -> x4, Pallas kernels: none -> 137 us  [the longest x1 59.9 us: local_layer(): pl.pallas_call(mlp_kernel, name='mlp', grid=(rows // mb,), in_specs=[pl.B...]
    ppermute x2 -> x25, waiting for transfers between devices: 0.01 us -> 64.7 us  [the longest x5 40.5 us: swap_tp(): return lax.ppermute(v, 'tp', flip['tp'])]
    reduce_sum x3 -> x0, other arithmetic: 51.1 us -> none  [the longest x1 22.5 us: local_layer(): win_exp.sum(axis=-1, keepdims=True) + glob_exp.sum(axis=-1, keepdims=True)]
    scatter x2 -> x0, local copies, waits for them, and re-layouts: 51.1 us -> none  [local_layer(): heads_out = win_out.at[slot_rows].set(glob_out, mode='drop')]
    ppermute x2 -> x25, starting transfers between devices: 5.92 us -> 24.1 us  [the longest x5 6.25 us: swap_tp(): return lax.ppermute(v, 'tp', flip['tp'])]
  transfers between devices with their start and end apart: 6 -> 25, of which waited for: 2 -> 6; matrix products, arithmetic and copies ran while one was open for 57% -> 16% of each run, Pallas kernels for 0% -> 27%
where the time goes in v1:
time: 282 us; the launch traced here: 281 us
  Pallas kernels  137 us (49%)
  waiting for transfers between devices  64.7 us (23%)
  matrix products  24.5 us (9%)
  starting transfers between devices  24.1 us (9%)
  local copies, waits for them, and re-layouts  16.3 us (6%)
  other arithmetic  14.2 us (5%)
    pallas_call x1, Pallas kernels, local_layer(): pl.pallas_call(mlp_kernel, name='mlp', grid=(rows // mb,), in_specs=[pl.B...  59.9 us
    pallas_call x2, Pallas kernels, local_layer(): pl.pallas_call(functools.partial(window_kernel, base, n_win), name='windo...  55 us
    ppermute x5, waiting for transfers between devices, swap_tp(): return lax.ppermute(v, 'tp', flip['tp'])  40.5 us
    dot_general x9, matrix products, dot(): return lax.dot_general(a, b, (dims, ((), ())), preferred_element_type=F32)  24.5 us
    ppermute x6, waiting for transfers between devices, swap_x(): return lax.ppermute(v, 'sp', flip[2])  22.6 us
    pallas_call x1, Pallas kernels, local_layer(): pl.pallas_call(glob_kernel, name='glob_attn', grid=(n_pairs, n_tiles), in...  22.4 us
    dynamic_slice x3, local copies, waits for them, and re-layouts, quarters(): mine = swap_tp(lax.dynamic_slice_in_dim(w, rank * size, size, axis))  6.27 us
    ppermute x5, starting transfers between devices, swap_tp(): return lax.ppermute(v, 'tp', flip['tp'])  6.25 us
  transfers between devices with their start and end apart: 25, of which 6 were waited for; matrix products, arithmetic and copies ran while one was open for 16% of the time, Pallas kernels for 27%

profile of v1, /device:TPU:0, one launch (start us, length us, event | category | flops | bytes accessed | tf_op | source)
XLA Modules:
  0.0 281.5 jit_solution(4330943637044515658)
XLA Ops:
  0.8 5.7 %fusion.4 = bf16[512,1024]{1,0:T(8,128)(2,1)} fusion(bf16[2048,1024]{1,0:T(8,128)(2,1)} %x_ref.1, s32[512]{0:T(512)S(1)} %broadcast_subtract_fusion), kind=kOutput, calls=%fused_computation.14 | convolution fusion | flops 2149056512 | bytes 5244928 | tf_op jit(solution)/shard_map/dot_general | solution.py:167
  7.3 2.4 convolution_convert_fusion.1.vt_ref
  12.0 3.8 %collective-permute-start.9 = (bf16[512,256]{1,0:T(8,128)(2,1)}, bf16[512,256]{1,0:T(8,128)(2,1)}, u32[]{:S(2)}, u32[]{:S(2)}) collective-permute-start(bf16[512,256]{1,0:T(8,128)(2,1)} %get-tuple-element.16), channel_id=1, source_target_pairs={{0,1},{1,2},{2,3},{4,5},{5,6},{6,7}} | collective-permute-start | bytes 786440 | tf_op jit(solution)/shard_map/ppermute | solution.py:200
  15.8 2.4 convolution_convert_fusion.2.k_ref
  20.4 3.3 %collective-permute-start.7 = (bf16[256,512]{1,0:T(8,128)(2,1)}, bf16[256,512]{1,0:T(8,128)(2,1)S(1)}, u32[]{:S(2)}, u32[]{:S(2)}) collective-permute-start(bf16[256,512]{1,0:T(8,128)(2,1)} %get-tuple-element.18), channel_id=1, source_target_pairs={{0,1},{1,2},{2,3},{4,5},{5,6},{6,7}} | collective-permute-start | bytes 786440 | tf_op jit(solution)/shard_map/ppermute | solution.py:198
  23.8 2.3 constant_dynamic-slice_fusion.1
  26.1 2.1 collective-permute-start.17
  28.3 6.3 %fusion.q_ref = bf16[512,2048]{1,0:T(8,128)(2,1)} fusion(bf16[1024,512]{1,0:T(8,128)(2,1)} %param.13, bf16[2048,1024]{1,0:T(8,128)(2,1)} %x_ref.1), kind=kOutput, calls=%fused_computation.4 | convolution fusion | flops 2149580800 | bytes 7340032 | tf_op jit(solution)/shard_map/dot_general | solution.py:167
  34.5 2.2 dynamic-slice_add_fusion
  37.2 2.3 constant_dynamic-slice_fusion
  39.5 1.8 fusion.2
  41.2 1.7 constant_dynamic-slice_fusion.2
  45.5 5.4 %collective-permute-done.1 = bf16[256,1024]{1,0:T(8,128)(2,1)} collective-permute-done((bf16[256,1024]{1,0:T(8,128)(2,1)}, bf16[256,1024]{1,0:T(8,128)(2,1)}, u32[]{:S(2)}, u32[]{:S(2)}) %collective-permute-start.1) | collective-permute-done | bytes 524320 | tf_op jit(solution)/shard_map/ppermute | solution.py:149
  56.6 2.7 pad_maximum_fusion.1.vt_ref
  59.3 21.7 %collective-permute-done.13.refs_0_ = bf16[128,1024]{1,0:T(8,128)(2,1)} collective-permute-done((bf16[128,1024]{1,0:T(8,128)(2,1)}, bf16[128,1024]{1,0:T(8,128)(2,1)}, u32[]{:S(2)}, u32[]{:S(2)}) %collective-permute-start.13) | collective-permute-done | bytes 262176 | tf_op jit(solution)/shard_map/ppermute | solution.py:143
  82.8 1.9 collective-permute-start.18
  86.5 22.4 %glob_attn.1 = (f32[512,512]{1,0:T(8,128)}, f32[16,8,256]{2,1,0:T(8,128)}, f32[16,8,256]{2,1,0:T(8,128)}) custom-call(bf16[512,512]{1,0:T(8,128)(2,1)} %fusion.9.q_ref, bf16[2048,512]{1,0:T(8,128)(2,1)} %copy-done.3, bf16[512,2048]{1,0:T(8,128)(2,1)} %copy-done.2), custom_call_target="tpu_custom_call" | custom-call | flops 16000000000 | bytes 8388608 | tf_op jit(solution)/shard_map/glob_attn/pallas_call | solution.py:203
  113.0 1.9 collective-permute-start.5
  116.5 17.2 %collective-permute-done.5 = f32[2,8,512]{2,1,0:T(8,128)S(1)} collective-permute-done((f32[2,8,512]{2,1,0:T(8,128)S(1)}, f32[2,8,512]{2,1,0:T(8,128)S(1)}, u32[]{:S(2)}, u32[]{:S(2)}) %collective-permute-start.5) | collective-permute-done | bytes 32800 | tf_op jit(solution)/shard_map/ppermute | solution.py:149
  134.3 27.5 %window_attn.2 = bf16[1024,512]{1,0:T(8,128)(2,1)} custom-call(s32[6]{0:T(128)} %stack.31.info_ref, bf16[512,2048]{1,0:T(8,128)(2,1)} %fusion.q_ref, bf16[2560,512]{1,0:T(8,128)(2,1)} %pad_maximum_fusion.k_ref, bf16[512,2560]{1,0:T(8,128)(2,1)} %pad_maximum_fusion.1.vt_ref, bf16[512,512]{1,0:T(8,128)(2,1)} %convolution_convert_fusion.6.kg_ref, ...), custom_call_target="tpu_custom_call" | custom-call | flops 16000000000 | bytes 8388608 | tf_op jit(solution)/shard_map/window_attn/pallas_call | solution.py:250
  165.7 27.5 %window_attn.3 = bf16[1024,512]{1,0:T(8,128)(2,1)} custom-call(s32[6]{0:T(128)} %stack.31.info_ref, bf16[512,2048]{1,0:T(8,128)(2,1)} %fusion.q_ref, bf16[2560,512]{1,0:T(8,128)(2,1)} %pad_maximum_fusion.k_ref, bf16[512,2560]{1,0:T(8,128)(2,1)} %pad_maximum_fusion.1.vt_ref, bf16[512,512]{1,0:T(8,128)(2,1)} %convolution_convert_fusion.6.kg_ref, ...), custom_call_target="tpu_custom_call" | custom-call | flops 16000000000 | bytes 8388608 | tf_op jit(solution)/shard_map/window_attn/pallas_call | solution.py:250
  193.2 2.2 fusion.6
  200.1 18.7 %collective-permute-done.12 = bf16[1024,512]{1,0:T(8,128)(2,1)S(1)} collective-permute-done((bf16[1024,512]{1,0:T(8,128)(2,1)S(1)}, bf16[1024,512]{1,0:T(8,128)(2,1)S(1)}, u32[]{:S(2)}, u32[]{:S(2)}) %collective-permute-start.12) | collective-permute-done | bytes 1048608 | tf_op jit(solution)/shard_map/ppermute | solution.py:143
  221.5 59.9 %mlp.1 = bf16[2048,1024]{1,0:T(8,128)(2,1)} custom-call(s32[6]{0:T(128)} %stack.31.info_ref, bf16[2048,1024]{1,0:T(8,128)(2,1)} %x_ref.1, bf16[2048,512]{1,0:T(8,128)(2,1)} %pad_maximum_fusion.2.oa_ref, bf16[2048,512]{1,0:T(8,128)(2,1)} %pad_maximum_fusion.3.ob_ref, bf16[512,1024]{1,0:T(8,128)(2,1)} %wo_ref.1, bf16[1024,2048]{1,0:T(8,128)(2,1)} %wu_ref.1, ...), custom_call_target="tpu_custom_call" | custom-call | flops 38000001024 | bytes 31457280 | tf_op jit(solution)/shard_map/mlp/pallas_call | solution.py:285
  (105 shorter events, 35.7 us)
Async XLA Ops:
  6.5 28.1 %collective-permute-start = (bf16[512,1024]{1,0:T(8,128)(2,1)}, bf16[512,1024]{1,0:T(8,128)(2,1)}, u32[]{:S(2)}, u32[]{:S(2)}) collective-permute-start(bf16[512,1024]{1,0:T(8,128)(2,1)} %fusion.4), channel_id=1, source_target_pairs={{0,1},{1,0},{2,3},{3,2},{4,5},{5,4},{6,7},{7,6}} | collective-permute-start | bytes 3145736 | tf_op jit(solution)/shard_map/ppermute | solution.py:146
  10.7 42.0 %collective-permute-start.10 = (bf16[512,256]{1,0:T(8,128)(2,1)}, bf16[512,256]{1,0:T(8,128)(2,1)}, u32[]{:S(2)}, u32[]{:S(2)}) collective-permute-start(bf16[512,256]{1,0:T(8,128)(2,1)} %get-tuple-element.17), channel_id=1, source_target_pairs={{1,0},{2,1},{3,2},{5,4},{6,5},{7,6}} | collective-permute-start | bytes 786440 | tf_op jit(solution)/shard_map/ppermute | solution.py:200
  12.0 42.2 %collective-permute-start.9 = (bf16[512,256]{1,0:T(8,128)(2,1)}, bf16[512,256]{1,0:T(8,128)(2,1)}, u32[]{:S(2)}, u32[]{:S(2)}) collective-permute-start(bf16[512,256]{1,0:T(8,128)(2,1)} %get-tuple-element.16), channel_id=1, source_target_pairs={{0,1},{1,2},{2,3},{4,5},{5,6},{6,7}} | collective-permute-start | bytes 786440 | tf_op jit(solution)/shard_map/ppermute | solution.py:200
  20.4 35.3 %collective-permute-start.7 = (bf16[256,512]{1,0:T(8,128)(2,1)}, bf16[256,512]{1,0:T(8,128)(2,1)S(1)}, u32[]{:S(2)}, u32[]{:S(2)}) collective-permute-start(bf16[256,512]{1,0:T(8,128)(2,1)} %get-tuple-element.18), channel_id=1, source_target_pairs={{0,1},{1,2},{2,3},{4,5},{5,6},{6,7}} | collective-permute-start | bytes 786440 | tf_op jit(solution)/shard_map/ppermute | solution.py:198
  26.1 56.7 %collective-permute-start.17 = (bf16[1024,512]{1,0:T(8,128)(2,1)}, bf16[1024,512]{1,0:T(8,128)(2,1)}, u32[]{:S(2)}, u32[]{:S(2)}) collective-permute-start(bf16[1024,512]{1,0:T(8,128)(2,1)} %constant_dynamic-slice_fusion.1), channel_id=1, source_target_pairs={{0,4},{4,0},{1,5},{5,1},{2,6},{6,2},{3,7},{7,3}} | collective-permute-start | bytes 3145736 | tf_op jit(solution)/shard_map/ppermute | solution.py:143
  36.7 14.1 %collective-permute-start.1 = (bf16[256,1024]{1,0:T(8,128)(2,1)}, bf16[256,1024]{1,0:T(8,128)(2,1)}, u32[]{:S(2)}, u32[]{:S(2)}) collective-permute-start(bf16[256,1024]{1,0:T(8,128)(2,1)} %dynamic-slice_add_fusion), channel_id=1, source_target_pairs={{0,2},{1,3},{2,0},{3,1},{4,6},{5,7},{6,4},{7,5}} | collective-permute-start | bytes 1572872 | tf_op jit(solution)/shard_map/ppermute | solution.py:149
  50.9 33.9 %collective-permute-start.21 = (bf16[512,1024]{1,0:T(8,128)(2,1)}, bf16[512,1024]{1,0:T(8,128)(2,1)}, u32[]{:S(2)}, u32[]{:S(2)}) collective-permute-start(bf16[512,1024]{1,0:T(8,128)(2,1)} %constant_dynamic-slice_fusion), channel_id=1, source_target_pairs={{0,4},{4,0},{1,5},{5,1},{2,6},{6,2},{3,7},{7,3}} | collective-permute-start | bytes 3145736 | tf_op jit(solution)/shard_map/ppermute | solution.py:143
  52.8 28.4 %collective-permute-start.8 = (bf16[256,512]{1,0:T(8,128)(2,1)}, bf16[256,512]{1,0:T(8,128)(2,1)S(1)}, u32[]{:S(2)}, u32[]{:S(2)}) collective-permute-start(bf16[256,512]{1,0:T(8,128)(2,1)} %get-tuple-element.19), channel_id=1, source_target_pairs={{1,0},{2,1},{3,2},{5,4},{6,5},{7,6}} | collective-permute-start | bytes 786440 | tf_op jit(solution)/shard_map/ppermute | solution.py:198
  54.2 26.8 %collective-permute-start.13 = (bf16[128,1024]{1,0:T(8,128)(2,1)}, bf16[128,1024]{1,0:T(8,128)(2,1)}, u32[]{:S(2)}, u32[]{:S(2)}) collective-permute-start(bf16[128,1024]{1,0:T(8,128)(2,1)} %constant_dynamic-slice_fusion.2), channel_id=1, source_target_pairs={{0,4},{4,0},{1,5},{5,1},{2,6},{6,2},{3,7},{7,3}} | collective-permute-start | bytes 786440 | tf_op jit(solution)/shard_map/ppermute | solution.py:143
  55.8 29.1 %collective-permute-start.2 = (bf16[256,1024]{1,0:T(8,128)(2,1)S(1)}, bf16[256,1024]{1,0:T(8,128)(2,1)S(1)}, u32[]{:S(2)}, u32[]{:S(2)}) collective-permute-start(bf16[256,1024]{1,0:T(8,128)(2,1)S(1)} %add.51), channel_id=1, source_target_pairs={{0,1},{1,0},{2,3},{3,2},{4,5},{5,4},{6,7},{7,6}} | collective-permute-start | bytes 1572872 | tf_op jit(solution)/shard_map/ppermute | solution.py:146
  81.1 115.0 %collective-permute-start.14 = (bf16[128,1024]{1,0:T(8,128)(2,1)}, bf16[128,1024]{1,0:T(8,128)(2,1)}, u32[]{:S(2)}, u32[]{:S(2)}) collective-permute-start(bf16[128,1024]{1,0:T(8,128)(2,1)} %collective-permute-done.13.refs_0_), channel_id=1, source_target_pairs={{0,2},{1,3},{2,0},{3,1},{4,6},{5,7},{6,4},{7,5}} | collective-permute-start | bytes 786440 | tf_op jit(solution)/shard_map/ppermute | solution.py:149
  82.8 114.9 %collective-permute-start.18 = (bf16[1024,512]{1,0:T(8,128)(2,1)}, bf16[1024,512]{1,0:T(8,128)(2,1)}, u32[]{:S(2)}, u32[]{:S(2)}) collective-permute-start(bf16[1024,512]{1,0:T(8,128)(2,1)} %collective-permute-done.17.refs_4_), channel_id=1, source_target_pairs={{0,2},{1,3},{2,0},{3,1},{4,6},{5,7},{6,4},{7,5}} | collective-permute-start | bytes 3145736 | tf_op jit(solution)/shard_map/ppermute | solution.py:149
  84.8 113.3 %collective-permute-start.22 = (bf16[512,1024]{1,0:T(8,128)(2,1)}, bf16[512,1024]{1,0:T(8,128)(2,1)}, u32[]{:S(2)}, u32[]{:S(2)}) collective-permute-start(bf16[512,1024]{1,0:T(8,128)(2,1)} %collective-permute-done.21.refs_8_), channel_id=1, source_target_pairs={{0,2},{1,3},{2,0},{3,1},{4,6},{5,7},{6,4},{7,5}} | collective-permute-start | bytes 3145736 | tf_op jit(solution)/shard_map/ppermute | solution.py:149
  110.9 2.1 collective-permute-start.3
  110.9 22.8 %collective-permute-start.4 = (f32[512,512]{1,0:T(8,128)}, f32[512,512]{1,0:T(8,128)S(1)}, u32[]{:S(2)}, u32[]{:S(2)}) collective-permute-start(f32[512,512]{1,0:T(8,128)} %get-tuple-element.8), channel_id=1, source_target_pairs={{0,1},{1,0},{2,3},{3,2},{4,5},{5,4},{6,7},{7,6}} | collective-permute-start | bytes 3145736 | tf_op jit(solution)/shard_map/ppermute | solution.py:146
  113.0 20.7 %collective-permute-start.5 = (f32[2,8,512]{2,1,0:T(8,128)S(1)}, f32[2,8,512]{2,1,0:T(8,128)S(1)}, u32[]{:S(2)}, u32[]{:S(2)}) collective-permute-start(f32[2,8,512]{2,1,0:T(8,128)S(1)} %pad_maximum_fusion.9), channel_id=1, source_target_pairs={{0,2},{1,3},{2,0},{3,1},{4,6},{5,7},{6,4},{7,5}} | collective-permute-start | bytes 98312 | tf_op jit(solution)/shard_map/ppermute | solution.py:149
  134.0 27.8 %collective-permute-start.6 = (f32[512,512]{1,0:T(8,128)S(1)}, f32[512,512]{1,0:T(8,128)S(1)}, u32[]{:S(2)}, u32[]{:S(2)}) collective-permute-start(f32[512,512]{1,0:T(8,128)S(1)} %fusion.12), channel_id=1, source_target_pairs={{0,2},{1,3},{2,0},{3,1},{4,6},{5,7},{6,4},{7,5}} | collective-permute-start | bytes 3145736 | tf_op jit(solution)/shard_map/ppermute | solution.py:149
  164.2 34.0 %collective-permute-start.11 = (bf16[1024,512]{1,0:T(8,128)(2,1)S(1)}, bf16[1024,512]{1,0:T(8,128)(2,1)S(1)}, u32[]{:S(2)}, u32[]{:S(2)}) collective-permute-start(bf16[1024,512]{1,0:T(8,128)(2,1)S(1)} %fusion.5), channel_id=1, source_target_pairs={{0,4},{4,0},{1,5},{5,1},{2,6},{6,2},{3,7},{7,3}} | collective-permute-start | bytes 3145736 | tf_op jit(solution)/shard_map/ppermute | solution.py:143
  195.5 23.3 %collective-permute-start.12 = (bf16[1024,512]{1,0:T(8,128)(2,1)S(1)}, bf16[1024,512]{1,0:T(8,128)(2,1)S(1)}, u32[]{:S(2)}, u32[]{:S(2)}) collective-permute-start(bf16[1024,512]{1,0:T(8,128)(2,1)S(1)} %fusion.6), channel_id=1, source_target_pairs={{0,4},{4,0},{1,5},{5,1},{2,6},{6,2},{3,7},{7,3}} | collective-permute-start | bytes 3145736 | tf_op jit(solution)/shard_map/ppermute | solution.py:143
  196.0 1.5 collective-permute-start.15
  197.6 22.8 %collective-permute-start.19 = (bf16[1024,512]{1,0:T(8,128)(2,1)}, bf16[1024,512]{1,0:T(8,128)(2,1)S(1)}, u32[]{:S(2)}, u32[]{:S(2)}) collective-permute-start(bf16[1024,512]{1,0:T(8,128)(2,1)} %collective-permute-done.17.refs_4_), channel_id=1, source_target_pairs={{0,1},{1,0},{2,3},{3,2},{4,5},{5,4},{6,7},{7,6}} | collective-permute-start | bytes 3145736 | tf_op jit(solution)/shard_map/ppermute | solution.py:146
  197.7 22.7 %collective-permute-start.23 = (bf16[512,1024]{1,0:T(8,128)(2,1)}, bf16[512,1024]{1,0:T(8,128)(2,1)}, u32[]{:S(2)}, u32[]{:S(2)}) collective-permute-start(bf16[512,1024]{1,0:T(8,128)(2,1)} %collective-permute-done.21.refs_8_), channel_id=1, source_target_pairs={{0,1},{1,0},{2,3},{3,2},{4,5},{5,4},{6,7},{7,6}} | collective-permute-start | bytes 3145736 | tf_op jit(solution)/shard_map/ppermute | solution.py:146
  198.1 22.3 %collective-permute-start.20 = (bf16[1024,512]{1,0:T(8,128)(2,1)}, bf16[1024,512]{1,0:T(8,128)(2,1)}, u32[]{:S(2)}, u32[]{:S(2)}) collective-permute-start(bf16[1024,512]{1,0:T(8,128)(2,1)} %collective-permute-done.18.refs_5_), channel_id=1, source_target_pairs={{0,1},{1,0},{2,3},{3,2},{4,5},{5,4},{6,7},{7,6}} | collective-permute-start | bytes 3145736 | tf_op jit(solution)/shard_map/ppermute | solution.py:146
  198.2 22.2 %collective-permute-start.24 = (bf16[512,1024]{1,0:T(8,128)(2,1)}, bf16[512,1024]{1,0:T(8,128)(2,1)}, u32[]{:S(2)}, u32[]{:S(2)}) collective-permute-start(bf16[512,1024]{1,0:T(8,128)(2,1)} %collective-permute-done.22.refs_9_), channel_id=1, source_target_pairs={{0,1},{1,0},{2,3},{3,2},{4,5},{5,4},{6,7},{7,6}} | collective-permute-start | bytes 3145736 | tf_op jit(solution)/shard_map/ppermute | solution.py:146
  (18 other events, 258.7 us)

commit v2 on v1

--- a/solution.py
+++ b/solution.py
@@ -11,6 +11,7 @@
 F32 = jnp.float32
 NEG = float("-inf")
 QB = 128
+MESH = pl.DeviceIdType.MESH
 
 
 def const_spec(shape):
@@ -91,12 +92,142 @@
         o_ref[:, lanes] = jnp.transpose(unpair(o_two)).astype(BF)
 
 
-def glob_kernel(q_ref, k_ref, vt_ref, o_ref, m_ref, l_ref, score):
-    rows = k_ref.shape[0]
+def front_kernel(n_seq, scale, x_ref, gpos_ref, wq_ref, wk_ref, wv_ref, wqg_ref, qt_ref, k_ref, vt_ref, kg_ref, vgt_ref, qgt_ref,
+                 x_send, x_half, x_in, x_in2, xg, send_sem, recv_sem):
+    rank = lax.axis_index("sp")
+    core = lax.rem(rank, 2)
+    mate = rank + 1 - 2 * core
+    across = lax.rem(rank + 2, n_seq)
+    rows, dim = x_ref.shape
+    half = gpos_ref.shape[0] // 2
+    halo = (k_ref.shape[0] - rows) // 2
+
+    barrier = pltpu.get_barrier_semaphore()
+    for step in range(1, n_seq):
+        pl.semaphore_signal(barrier, inc=1, device_id={"sp": lax.rem(rank + step, n_seq)}, device_id_type=MESH)
+    pl.semaphore_wait(barrier, n_seq - 1)
+
+    def copy(src, dst, idx, dev):
+        return pltpu.make_async_remote_copy(
+            src_ref=src, dst_ref=dst, send_sem=send_sem.at[idx], recv_sem=recv_sem.at[idx],
+            device_id={"sp": dev}, device_id_type=MESH)
+
+    def dot(a, b, dims):
+        return lax.dot_general(a, b, (dims, ((), ())), preferred_element_type=F32)
+
+    def picked(which):
+        slots = gpos_ref[pl.ds(pl.multiple_of(which * half, half), half), :] - rank * rows
+        acc = None
+        for c in range(rows // 512):
+            at = lax.broadcasted_iota(jnp.int32, (half, 512), 1) + 512 * c
+            hot = jnp.where(slots == at, 1.0, 0.0).astype(BF)
+            part = dot(hot, x_ref[512 * c:512 * c + 512, :], ((1,), (0,)))
+            acc = part if acc is None else acc + part
+        return acc.astype(BF)
+
+    x_send[...] = picked(1 - core)
+    first = copy(x_send, x_in, 0, mate)
+    mine = picked(core)
+    x_half[...] = mine
+    first.start()
+
+    def keys(c):
+        at = pl.ds(pl.multiple_of(c * 256, 256), 256)
+        k_ref[pl.ds(pl.multiple_of(halo + c * 256, 256), 256), :] = dot(x_ref[at, :], wk_ref[...], ((1,), (0,))).astype(BF)
+
+    def values(c):
+        at = pl.ds(pl.multiple_of(c * 256, 256), 256)
+        vt_ref[:, pl.ds(pl.multiple_of(halo + c * 256, 256), 256)] = dot(wv_ref[...], x_ref[at, :], ((0,), (1,))).astype(BF)
+
+    def queries(c):
+        at = pl.ds(pl.multiple_of(c * 256, 256), 256)
+        qt_ref[:, at] = dot(wq_ref[...], x_ref[at, :], ((0,), (1,))).astype(BF) * BF(scale)
+
+    n_blk = rows // 256
+    keys(0)
+    keys(n_blk - 1)
+    first.wait()
+    x_half[...] = x_half[...] + x_in[...]
+    values(0)
+    second = copy(x_half, x_in2, 1, across)
+    second.start()
+    values(n_blk - 1)
+    to_right = [
+        copy(k_ref.at[pl.ds(rows, halo), :], k_ref.at[pl.ds(0, halo), :], 2, rank + 1),
+        copy(vt_ref.at[:, pl.ds(rows, halo)], vt_ref.at[:, pl.ds(0, halo)], 3, rank + 1)]
+    to_left = [
+        copy(k_ref.at[pl.ds(halo, halo), :], k_ref.at[pl.ds(halo + rows, halo), :], 4, rank - 1),
+        copy(vt_ref.at[:, pl.ds(halo, halo)], vt_ref.at[:, pl.ds(halo + rows, halo)], 5, rank - 1)]
+
+    def later(c, carry):
+        keys(c)
+        values(c)
+        return carry
+
+    @pl.when(rank < n_seq - 1)
+    def _():
+        for c in to_right:
+            c.start()
+
+    @pl.when(rank > 0)
+    def _():
+        for c in to_left:
+            c.start()
+
+    lax.fori_loop(1, n_blk - 1, later, 0)
+    lax.fori_loop(0, n_blk, lambda c, carry: (queries(c), carry)[1], 0)
+
+    second.wait()
+    own = pl.ds(pl.multiple_of(core * half, half), half)
+    other = pl.ds(pl.multiple_of((1 - core) * half, half), half)
+    xg[own, :] = x_half[...] + x_in2[...]
+
+    def project(at):
+        kg_ref[at, :] = dot(xg[at, :], wk_ref[...], ((1,), (0,))).astype(BF)
+        vgt_ref[:, at] = dot(wv_ref[...], xg[at, :], ((0,), (1,))).astype(BF)
+
+    def project_query(at):
+        qgt_ref[:, at] = dot(wqg_ref[...], xg[at, :], ((0,), (1,))).astype(BF) * BF(scale)
+
+    third = copy(xg.at[own, :], xg.at[own, :], 6, mate)
+    project_query(own)
+    third.start()
+    project(own)
+    third.wait()
+    project_query(other)
+    project(other)
+
+    @pl.when(rank < n_seq - 1)
+    def _():
+        for c in to_right:
+            c.wait_send()
+        for c in to_left:
+            c.wait_recv()
+
+    @pl.when(rank > 0)
+    def _():
+        for c in to_left:
+            c.wait_send()
+        for c in to_right:
+            c.wait_recv()
+
+    @pl.when(rank == 0)
+    def _():
+        k_ref[0:halo, :] = jnp.zeros((halo, k_ref.shape[1]), BF)
+        vt_ref[:, 0:halo] = jnp.zeros((vt_ref.shape[0], halo), BF)
+
+    @pl.when(rank == n_seq - 1)
+    def _():
+        k_ref[halo + rows:, :] = jnp.zeros((halo, k_ref.shape[1]), BF)
+        vt_ref[:, halo + rows:] = jnp.zeros((vt_ref.shape[0], halo), BF)
+
+
+def glob_kernel(halo, q_ref, k_ref, vt_ref, o_ref, m_ref, l_ref, score):
+    rows = k_ref.shape[0] - 2 * halo
     rhs = pair_rhs(q_ref[...])
     top = None
     for c in range(rows // 256):
-        s = jnp.dot(k_ref[256 * c:256 * c + 256, :], rhs, preferred_element_type=F32)
+        s = jnp.dot(k_ref[halo + 256 * c:halo + 256 * c + 256, :], rhs, preferred_element_type=F32)
         score[256 * c:256 * c + 256, :] = s
         part = jnp.max(s.reshape(32, 8, 2 * QB), axis=0)
         top = part if top is None else jnp.maximum(top, part)
@@ -107,36 +238,72 @@
         e = jnp.exp(score[256 * c:256 * c + 256, :] - top)
         part = jnp.sum(e.reshape(32, 8, 2 * QB), axis=0)
         total = part if total is None else total + part
-        o = jnp.dot(vt_ref[:, 256 * c:256 * c + 256], e.astype(BF), preferred_element_type=F32)
+        o = jnp.dot(vt_ref[:, halo + 256 * c:halo + 256 * c + 256], e.astype(BF), preferred_element_type=F32)
         acc = o if acc is None else acc + o
     o_ref[...] = unpair(acc)
     m_ref[0] = jnp.broadcast_to(top, (8, 2 * QB))
     l_ref[0] = jnp.broadcast_to(jnp.sum(total, axis=0, keepdims=True), (8, 2 * QB))
 
 
-def mlp_kernel(info_ref, x_ref, oa_ref, ob_ref, wo_ref, wu_ref, wd_ref, *refs):
-    wo_p, wu_p, wd_p, out_ref = refs[0:4], refs[4:8], refs[8:12], refs[12]
-    piece = wu_p[0].shape[1]
-    acc = x_ref[...].astype(F32) + jnp.dot(oa_ref[...], wo_ref[...], preferred_element_type=F32)
+def mlp_kernel(info_ref, x_ref, oa_ref, ob_ref, wo_hbm, wu_hbm, wd_hbm, p0, p1, p2, p3, out_ref, wo, wu, wd, pk, sem):
+    packs = (p0, p1, p2, p3)
+    first = pl.program_id(0) == 0
+    dim = wu.shape[0]
+    piece = pk.shape[2]
+    n_col = dim // piece
+    depth = wo.shape[0] // 4
+    head = dim + piece * n_col
+
+    def part(src, dst, idx):
+        return pltpu.make_async_copy(src, dst, sem.at[idx])
+
+    loads = {"wo": part(wo_hbm, wo, 0)}
     for k in range(4):
-        depth = wo_p[k].shape[0]
-        cols = pl.ds(pl.multiple_of(info_ref[2 + k] * depth, depth), depth)
-        acc = acc + jnp.dot(ob_ref[:, cols], wo_p[k][...], preferred_element_type=F32)
-    h = acc.astype(BF)
+        cols = pl.ds(k * piece, piece)
+        loads["po", k] = part(packs[k].at[pl.ds(head, depth * n_col), :], pk.at[k, pl.ds(head, depth * n_col), :], 1 + k)
+        loads["u", k] = part(wu_hbm.at[:, cols], wu.at[:, cols], 5 + k)
+        loads["d", k] = part(wd_hbm.at[cols, :], wd.at[cols, :], 9 + k)
+        loads["p", k] = part(packs[k].at[pl.ds(0, head), :], pk.at[k, pl.ds(0, head), :], 13 + k)
+
+    @pl.when(first)
+    def _():
+        for c in loads.values():
+            c.start()
+
+    def ready(*key):
+        @pl.when(first)
+        def _():
+            for k in key:
+                loads[k].wait()
+
+    ready("wo", ("po", 0), ("po", 1), ("po", 2), ("po", 3))
+    acc = x_ref[...].astype(F32) + jnp.dot(oa_ref[...], wo[...], preferred_element_type=F32)
+    extra = [None] * n_col
+    for k in range(4):
+        o = ob_ref[:, pl.ds(pl.multiple_of(info_ref[2 + k] * depth, depth), depth)]
+        for c in range(n_col):
+            t = jnp.dot(o, pk[k, head + c * depth:head + (c + 1) * depth, :], preferred_element_type=F32)
+            extra[c] = t if extra[c] is None else extra[c] + t
+    h = (acc + jnp.concatenate(extra, axis=1)).astype(BF)
     acc = h.astype(F32)
     for k in range(8):
-        cols = slice(piece * (k % 4), piece * (k % 4) + piece)
-        up = wu_ref[:, cols] if k < 4 else wu_p[k - 4][...]
-        down = wd_ref[cols, :] if k < 4 else wd_p[k - 4][...]
+        if k < 4:
+            ready(("u", k), ("d", k))
+            up = wu[:, k * piece:(k + 1) * piece]
+        else:
+            ready(("p", k - 4))
+            up = pk[k - 4, :dim, :]
         act = jax.nn.gelu(jnp.dot(h, up, preferred_element_type=F32)).astype(BF)
-        acc = acc + jnp.dot(act, down, preferred_element_type=F32)
+        if k < 4:
+            acc = acc + jnp.dot(act, wd[k * piece:(k + 1) * piece, :], preferred_element_type=F32)
+        else:
+            parts = [jnp.dot(act, pk[k - 4, dim + c * piece:dim + (c + 1) * piece, :], preferred_element_type=F32) for c in range(n_col)]
+            acc = acc + jnp.concatenate(parts, axis=1)
     out_ref[...] = acc.astype(BF)
 
 
 def solution(mesh):
     n_seq = mesh.shape["sp"]
-    to_right = [(s, s + 1) for s in range(n_seq - 1)]
-    to_left = [(s + 1, s) for s in range(n_seq - 1)]
     flip = {"tp": [(0, 1), (1, 0)], 1: [(s, s ^ 1) for s in range(n_seq)], 2: [(s, s ^ 2) for s in range(n_seq)]}
 
     def swap_tp(v):
@@ -159,55 +326,53 @@
         n_win = 2 * window // 128 + 1
         scale = head_dim ** -0.5
         rank = lax.axis_index("sp")
-        core = rank % 2
         row_start = rank * rows
         vmem = 60 * 1024 * 1024
 
         def dot(a, b, dims):
             return lax.dot_general(a, b, (dims, ((), ())), preferred_element_type=F32)
 
-        def quarters(w, axis):
+        def quarter(w, axis):
             size = w.shape[axis] // n_seq
-            mine = swap_tp(lax.dynamic_slice_in_dim(w, rank * size, size, axis))
-            across = swap_x(mine)
-            return [mine, across, swap_core(mine), swap_core(across)]
-
-        wo_p = quarters(w_out, 0)
-        wu_p = quarters(w_up, 1)
-        wd_p = quarters(w_down, 0)
+            return lax.dynamic_slice_in_dim(w, rank * size, size, axis)
+
+        piece = w_up.shape[1] // n_seq
+        pack = [quarter(w_up, 1)]
+        for w in (quarter(w_down, 0), quarter(w_out, 0)):
+            pack += [w[:, c * piece:(c + 1) * piece] for c in range(dim // piece)]
+        mine = swap_tp(jnp.concatenate(pack, axis=0))
+        far = swap_x(mine)
+        packs = [mine, far, swap_core(mine), swap_core(far)]
 
         slot = glob_pos - row_start
         pick = (slot[:, None] == jnp.arange(rows)[None, :]).astype(BF)
-        x_glob = dot(pick, tokens, ((1,), (0,))).astype(BF)
-        x_glob = x_glob + swap_core(x_glob)
+        n_ext = rows + 2 * window
         half = n_glob // 2
-        x_half = lax.dynamic_slice_in_dim(x_glob, core * half, half, 0)
-        x_half = x_half + swap_x(x_half)
-        x_other = swap_core(x_half)
-        first = core == 0
-        x_glob = jnp.concatenate([jnp.where(first, x_half, x_other), jnp.where(first, x_other, x_half)], axis=0)
-
-        q_t = dot(w_query, tokens, ((0,), (1,))).astype(BF) * BF(scale)
-        k_loc = dot(tokens, w_key, ((1,), (0,))).astype(BF)
-        v_t = dot(w_value, tokens, ((0,), (1,))).astype(BF)
-        kg = dot(x_glob, w_key, ((1,), (0,))).astype(BF)
-        vg_t = dot(w_value, x_glob, ((0,), (1,))).astype(BF)
-        qg_t = dot(w_query_glob, x_glob, ((0,), (1,))).astype(BF) * BF(scale)
-
-        k_ext = jnp.concatenate([
-            lax.ppermute(k_loc[rows - window:], "sp", to_right), k_loc, lax.ppermute(k_loc[:window], "sp", to_left)], axis=0)
-        v_ext = jnp.concatenate([
-            lax.ppermute(v_t[:, rows - window:], "sp", to_right), v_t, lax.ppermute(v_t[:, :window], "sp", to_left)], axis=1)
+        vm = pl.BlockSpec(memory_space=pltpu.VMEM)
+        q_t, k_ext, v_ext, kg, vg_t, qg_t = pl.pallas_call(
+            functools.partial(front_kernel, n_seq, scale),
+            name="front",
+            in_specs=[vm] * 6,
+            out_specs=[vm] * 6,
+            out_shape=[jax.ShapeDtypeStruct(sh, BF) for sh in (
+                (loc, rows), (n_ext, loc), (loc, n_ext), (n_glob, loc), (loc, n_glob), (loc, n_glob))],
+            scratch_shapes=[
+                pltpu.VMEM((half, dim), BF), pltpu.VMEM((half, dim), BF), pltpu.VMEM((half, dim), BF),
+                pltpu.VMEM((half, dim), BF), pltpu.VMEM((n_glob, dim), BF),
+                pltpu.SemaphoreType.DMA((7,)), pltpu.SemaphoreType.DMA((7,))],
+            compiler_params=pltpu.CompilerParams(vmem_limit_bytes=vmem, collective_id=0, has_side_effects=True),
+            cost_estimate=pl.CostEstimate(flops=16 * 10**9, bytes_accessed=16 * 2**20, transcendentals=0),
+        )(tokens, glob_pos[:, None], w_query, w_key, w_value, w_query_glob)
 
         n_tiles = n_glob // QB
         part_o, part_m, part_l = pl.pallas_call(
-            glob_kernel,
+            functools.partial(glob_kernel, window),
             name="glob_attn",
             grid=(n_pairs, n_tiles),
             in_specs=[
                 pl.BlockSpec((128, QB), lambda p, t: (p, t)),
-                pl.BlockSpec((rows, 128), lambda p, t: (0, p)),
-                pl.BlockSpec((128, rows), lambda p, t: (p, 0)),
+                pl.BlockSpec((n_ext, 128), lambda p, t: (0, p)),
+                pl.BlockSpec((128, n_ext), lambda p, t: (p, 0)),
             ],
             out_specs=[
                 pl.BlockSpec((128, QB), lambda p, t: (p, t)),
@@ -222,25 +387,25 @@
             scratch_shapes=[pltpu.VMEM((rows, 2 * QB), F32)],
             compiler_params=pltpu.CompilerParams(vmem_limit_bytes=vmem),
             cost_estimate=pl.CostEstimate(flops=16 * 10**9, bytes_accessed=8 * 2**20, transcendentals=heads * n_glob * rows),
-        )(qg_t, k_loc, v_t)
+        )(qg_t, k_ext, v_ext)
 
         def stat(s):
             s = s[:, 0, :].reshape(n_pairs, n_tiles, 2, QB)
             return s.transpose(0, 2, 1, 3).reshape(heads, n_glob)
 
-        stats = jnp.stack([stat(part_m), stat(part_l)])
+        shape = (heads, head_dim, n_glob)
+        m_all, l_all = stat(part_m), stat(part_l)
         for swap in (swap_core, swap_x):
-            o_far, s_far = swap(part_o), swap(stats)
-            top = jnp.maximum(stats[0], s_far[0])
-            mine, theirs = jnp.exp(stats[0] - top), jnp.exp(s_far[0] - top)
-            stats = jnp.stack([top, stats[1] * mine + s_far[1] * theirs])
-            shape = (heads, head_dim, n_glob)
-            part_o = (part_o.reshape(shape) * mine[:, None] + o_far.reshape(shape) * theirs[:, None]).reshape(loc, n_glob)
-        glob_o = (part_o.reshape(heads, head_dim, n_glob) / stats[1][:, None]).astype(BF).reshape(loc, n_glob)
+            far = swap(jnp.concatenate([part_o, m_all, l_all], axis=0))
+            m_far = far[loc:loc + heads]
+            top = jnp.maximum(m_all, m_far)
+            mine, theirs = jnp.exp(m_all - top), jnp.exp(m_far - top)
+            m_all, l_all = top, l_all * mine + far[loc + heads:] * theirs
+            part_o = (part_o.reshape(shape) * mine[:, None] + far[:loc].reshape(shape) * theirs[:, None]).reshape(loc, n_glob)
+        glob_o = (part_o.reshape(shape) / l_all[:, None]).astype(BF).reshape(loc, n_glob)
 
         br = jnp.pad(rel_bias[:, ::-1], ((0, 0), (128, 127)), constant_values=NEG)
         info = jnp.stack([row_start, jnp.int32(rows * n_seq), rank, rank ^ 2, rank ^ 1, rank ^ 3]).astype(jnp.int32)
-        n_ext = rows + 2 * window
         n_calls = 2
         blocks = rows // QB // n_calls
         is_glob = (slot[:, None] == jnp.arange(rows)[None, :]).any(axis=0)
@@ -281,7 +446,6 @@
 
         mb = 256
         hid = w_up.shape[1]
-        piece = hid // n_seq
         return pl.pallas_call(
             mlp_kernel,
             name="mlp",
@@ -291,18 +455,16 @@
                 pl.BlockSpec((mb, dim), lambda j: (j, 0)),
                 pl.BlockSpec((mb, loc), lambda j: (j, 0)),
                 pl.BlockSpec((mb, loc), lambda j: (j, 0)),
-                const_spec((loc, dim)),
-                const_spec((dim, hid)),
-                const_spec((hid, dim)),
-                *[const_spec((loc // n_seq, dim))] * 4,
-                *[const_spec((dim, piece))] * 4,
-                *[const_spec((piece, dim))] * 4,
+                *[pl.BlockSpec(memory_space=pl.ANY)] * 7,
             ],
             out_specs=pl.BlockSpec((mb, dim), lambda j: (j, 0)),
             out_shape=jax.ShapeDtypeStruct((rows, dim), BF),
+            scratch_shapes=[
+                pltpu.VMEM((loc, dim), BF), pltpu.VMEM((dim, hid), BF), pltpu.VMEM((hid, dim), BF),
+                pltpu.VMEM((4,) + packs[0].shape, BF), pltpu.SemaphoreType.DMA((17,))],
             compiler_params=pltpu.CompilerParams(vmem_limit_bytes=vmem),
             cost_estimate=pl.CostEstimate(flops=38 * 10**9, bytes_accessed=30 * 2**20, transcendentals=rows * hid * 2),
-        )(info, tokens, oa, ob, w_out, w_up, w_down, *wo_p, *wu_p, *wd_p)
+        )(info, tokens, oa, ob, w_out, w_up, w_down, *packs)
 
     row_spec = P(("batch", "sp"), None)
     col_spec = P(None, "tp")

time: 282 us -> 293 us (1.039)
  Pallas kernels: 137 us -> 173 us
  waiting for transfers between devices: 64.7 us -> 87.9 us
  matrix products: 24.5 us -> 1.72 us
  starting transfers between devices: 24.1 us -> 9.72 us
  other arithmetic: 14.2 us -> 6.78 us
    pallas_call x1 -> x2, Pallas kernels: 22.4 us -> 52.2 us  [the longest x1 29.8 us: local_layer(): pl.pallas_call(functools.partial(front_kernel, n_seq, scale), name='front...]
    ppermute x6 -> x2, waiting for transfers between devices: 22.6 us -> 45.5 us  [swap_x(): return lax.ppermute(v, 'sp', flip[2])]
    dot_general x9 -> x2, matrix products: 24.5 us -> 1.72 us  [dot(): return lax.dot_general(a, b, (dims, ((), ())), preferred_element_type=F32)]
    ppermute x4 -> x0, starting transfers between devices: 9.78 us -> none  [the longest x1 3.75 us: local_layer(): lax.ppermute(v_t[:, rows - window:], 'sp', to_right)]
    dynamic_slice x3 -> x0, local copies, waits for them, and re-layouts: 6.27 us -> none  [quarters(): mine = swap_tp(lax.dynamic_slice_in_dim(w, rank * size, size, axis))]
    pallas_call x1, Pallas kernels: 59.9 us -> 65.5 us  [local_layer(): pl.pallas_call(mlp_kernel, name='mlp', grid=(rows // mb,), in_specs=[pl.B...]
    unnamed x36 -> x16, local copies, waits for them, and re-layouts: 4.16 us -> 8.03 us
    add x3 -> x2, other arithmetic: 3.62 us -> 0.03 us  [local_layer(): m_all, l_all = (top, l_all * mine + far[loc + heads:] * theirs)]
  transfers between devices with their start and end apart: 25 -> 8, of which waited for: 6 -> 4; matrix products, arithmetic and copies ran while one was open for 16% -> 4% of each run, Pallas kernels for 27% -> 37%
where the time goes in v2:
time: 293 us
  Pallas kernels  173 us (59%)
  waiting for transfers between devices  87.9 us (30%)
  local copies, waits for them, and re-layouts  13.6 us (5%)
  starting transfers between devices  9.72 us (3%)
  other arithmetic  6.78 us (2%)
    pallas_call x1, Pallas kernels, local_layer(): pl.pallas_call(mlp_kernel, name='mlp', grid=(rows // mb,), in_specs=[pl.B...  65.5 us
    pallas_call x2, Pallas kernels, local_layer(): pl.pallas_call(functools.partial(window_kernel, base, n_win), name='windo...  55.1 us
    ppermute x2, waiting for transfers between devices, swap_x(): return lax.ppermute(v, 'sp', flip[2])  45.5 us
    ppermute x3, waiting for transfers between devices, swap_tp(): return lax.ppermute(v, 'tp', flip['tp'])  42.3 us
    pallas_call x1, Pallas kernels, local_layer(): pl.pallas_call(functools.partial(front_kernel, n_seq, scale), name='front...  29.8 us
    pallas_call x1, Pallas kernels, local_layer(): pl.pallas_call(functools.partial(glob_kernel, window), name='glob_attn',...  22.4 us
    unnamed x16, local copies, waits for them, and re-layouts  8.03 us
  transfers between devices with their start and end apart: 8, of which 4 were waited for; matrix products, arithmetic and copies ran while one was open for 4% of the time, Pallas kernels for 37%

profile of v2, /device:TPU:0, one launch (start us, length us, event | category | flops | bytes accessed | tf_op | source)
XLA Modules:
  0.0 292.8 jit_solution(16763593420274432144)
XLA Ops:
  0.0 2.3 dynamic-slice_dynamic-update-slice_fusion
  2.3 1.9 dynamic-slice_dynamic-update-slice_fusion.2
  4.1 1.9 dynamic-slice_dynamic-update-slice_fusion.1
  6.0 1.6 dynamic-slice_dynamic-update-slice_fusion.4
  7.6 1.6 dynamic-slice_dynamic-update-slice_fusion.3
  9.1 3.4 %collective-permute-start.4 = (bf16[2304,512]{1,0:T(8,128)(2,1)}, bf16[2304,512]{1,0:T(8,128)(2,1)}, u32[]{:S(2)}, u32[]{:S(2)}) collective-permute-start(bf16[2304,512]{1,0:T(8,128)(2,1)} %dynamic-slice_dynamic-update-slice_fusion.3), channel_id=1, source_target_pairs={{0,4},{4,0},{1,5},{5,1},{2,6},{6,2},{3,7},{7,3}} | collective-permute-start | bytes 7077896 | tf_op jit(solution)/shard_map/ppermute | solution.py:310
  12.5 0.9 copy.18.gpos_ref
  13.4 29.8 %front.1 = (bf16[512,2048]{1,0:T(8,128)(2,1)}, bf16[2560,512]{1,0:T(8,128)(2,1)}, bf16[512,2560]{1,0:T(8,128)(2,1)}, bf16[512,512]{1,0:T(8,128)(2,1)}, bf16[512,...) custom-call(bf16[2048,1024]{1,0:T(8,128)(2,1)} %x_ref.3, s32[512,1]{1,0:T(8,128)} %copy.18.gpos_ref, bf16[1024,512]{1,0:T(8,128)(2,1)} %wq_ref.1, ...), custom_call_target="tpu_custom_call" | custom-call | flops 16000000000 | bytes 16777216 | tf_op jit(solution)/shard_map/front/pallas_call | solution.py:352
  43.2 22.4 %glob_attn.1 = (f32[512,512]{1,0:T(8,128)}, f32[16,8,256]{2,1,0:T(8,128)}, f32[16,8,256]{2,1,0:T(8,128)}) custom-call(bf16[512,512]{1,0:T(8,128)(2,1)} %get-tuple-element.14.q_ref, bf16[2560,512]{1,0:T(8,128)(2,1)} %get-tuple-element.15.k_ref, bf16[512,2560]{1,0:T(8,128)(2,1)} %get-tuple-element.16.vt_ref), custom_call_target="tpu_custom_call" | custom-call | flops 16000000000 | bytes 8388608 | tf_op jit(solution)/shard_map/glob_attn/pallas_call | solution.py:368
  65.6 0.9 slice.50
  66.5 0.9 slice.51
  67.4 2.3 pad_maximum_fusion.2
  69.8 2.2 collective-permute-start
  73.7 27.5 %window_attn.2 = bf16[1024,512]{1,0:T(8,128)(2,1)} custom-call(s32[6]{0:T(128)} %stack.23.info_ref, bf16[512,2048]{1,0:T(8,128)(2,1)} %get-tuple-element.20.q_ref, bf16[2560,512]{1,0:T(8,128)(2,1)} %get-tuple-element.15.k_ref, bf16[512,2560]{1,0:T(8,128)(2,1)} %get-tuple-element.16.vt_ref, bf16[512,512]{1,0:T(8,128)(2,1)} %get-tuple-element.21.kg_ref, ...), custom_call_target="tpu_custom_call" | custom-call | flops 16000000000 | bytes 8388608 | tf_op jit(solution)/shard_map/window_attn/pallas_call | solution.py:415
  101.3 1.3 collective-permute-start.5
  103.7 27.5 %window_attn.3 = bf16[1024,512]{1,0:T(8,128)(2,1)} custom-call(s32[6]{0:T(128)} %stack.23.info_ref, bf16[512,2048]{1,0:T(8,128)(2,1)} %get-tuple-element.20.q_ref, bf16[2560,512]{1,0:T(8,128)(2,1)} %get-tuple-element.15.k_ref, bf16[512,2560]{1,0:T(8,128)(2,1)} %get-tuple-element.16.vt_ref, bf16[512,512]{1,0:T(8,128)(2,1)} %get-tuple-element.21.kg_ref, ...), custom_call_target="tpu_custom_call" | custom-call | flops 16000000000 | bytes 8388608 | tf_op jit(solution)/shard_map/window_attn/pallas_call | solution.py:415
  132.1 23.3 %collective-permute-done.5.p1 = bf16[2304,512]{1,0:T(8,128)(2,1)} collective-permute-done((bf16[2304,512]{1,0:T(8,128)(2,1)}, bf16[2304,512]{1,0:T(8,128)(2,1)}, u32[]{:S(2)}, u32[]{:S(2)}) %collective-permute-start.5) | collective-permute-done | bytes 2359328 | tf_op jit(solution)/shard_map/ppermute | solution.py:316
  155.4 22.2 %collective-permute-done.1 = f32[528,512]{1,0:T(8,128)S(1)} collective-permute-done((f32[528,512]{1,0:T(8,128)S(1)}, f32[528,512]{1,0:T(8,128)S(1)}, u32[]{:S(2)}, u32[]{:S(2)}) %collective-permute-start.1) | collective-permute-done | bytes 1081376 | tf_op jit(solution)/shard_map/ppermute | solution.py:316
  180.2 1.6 collective-permute-start.3
  181.8 1.4 pad_maximum_fusion.oa_ref
  183.2 21.7 %collective-permute-done.2 = bf16[1024,512]{1,0:T(8,128)(2,1)S(1)} collective-permute-done((bf16[1024,512]{1,0:T(8,128)(2,1)S(1)}, bf16[1024,512]{1,0:T(8,128)(2,1)S(1)}, u32[]{:S(2)}, u32[]{:S(2)}) %collective-permute-start.2) | collective-permute-done | bytes 1048608 | tf_op jit(solution)/shard_map/ppermute | solution.py:310
  204.9 20.7 %collective-permute-done.3 = bf16[1024,512]{1,0:T(8,128)(2,1)S(1)} collective-permute-done((bf16[1024,512]{1,0:T(8,128)(2,1)S(1)}, bf16[1024,512]{1,0:T(8,128)(2,1)S(1)}, u32[]{:S(2)}, u32[]{:S(2)}) %collective-permute-start.3) | collective-permute-done | bytes 1048608 | tf_op jit(solution)/shard_map/ppermute | solution.py:310
  225.6 1.5 pad_maximum_fusion.1.ob_ref
  227.1 65.5 %mlp.1 = bf16[2048,1024]{1,0:T(8,128)(2,1)} custom-call(s32[6]{0:T(128)} %stack.23.info_ref, bf16[2048,1024]{1,0:T(8,128)(2,1)} %x_ref.3, bf16[2048,512]{1,0:T(8,128)(2,1)} %pad_maximum_fusion.oa_ref, bf16[2048,512]{1,0:T(8,128)(2,1)} %pad_maximum_fusion.1.ob_ref, bf16[512,1024]{1,0:T(8,128)(2,1)} %wo_hbm.1, bf16[1024,2048]{1,0:T(8,128)(2,1)} %wu_hbm.1, ...), custom_call_target="tpu_custom_call" | custom-call | flops 38000001024 | bytes 31457280 | tf_op jit(solution)/shard_map/mlp/pallas_call | solution.py:449
  (35 shorter events, 6.3 us)
Async XLA Ops:
  0.0 12.5 %copy-start.2 = (s32[512]{0:T(512)S(1)}, s32[512]{0:T(512)}, u32[]{:S(2)}) copy-start(s32[512]{0:T(512)} %param.11) | copy-start | bytes 6148
  9.1 92.1 %collective-permute-start.4 = (bf16[2304,512]{1,0:T(8,128)(2,1)}, bf16[2304,512]{1,0:T(8,128)(2,1)}, u32[]{:S(2)}, u32[]{:S(2)}) collective-permute-start(bf16[2304,512]{1,0:T(8,128)(2,1)} %dynamic-slice_dynamic-update-slice_fusion.3), channel_id=1, source_target_pairs={{0,4},{4,0},{1,5},{5,1},{2,6},{6,2},{3,7},{7,3}} | collective-permute-start | bytes 7077896 | tf_op jit(solution)/shard_map/ppermute | solution.py:310
  65.6 6.4 %copy-start.1 = (f32[8,513]{1,0:T(8,128)S(1)}, f32[8,513]{1,0:T(8,128)}, u32[]{:S(2)}) copy-start(f32[8,513]{1,0:T(8,128)} %param.12) | copy-start | bytes 49252
  69.8 32.8 %collective-permute-start = (f32[528,512]{1,0:T(8,128)}, f32[528,512]{1,0:T(8,128)S(1)}, u32[]{:S(2)}, u32[]{:S(2)}) collective-permute-start(f32[528,512]{1,0:T(8,128)} %pad_maximum_fusion.2), channel_id=1, source_target_pairs={{0,1},{1,0},{2,3},{3,2},{4,5},{5,4},{6,7},{7,6}} | collective-permute-start | bytes 3244040 | tf_op jit(solution)/shard_map/ppermute | solution.py:313
  73.7 28.9 %copy-start = (f32[512,512]{1,0:T(8,128)S(1)}, f32[512,512]{1,0:T(8,128)}, u32[]{:S(2)}) copy-start(f32[512,512]{1,0:T(8,128)} %get-tuple-element.17) | copy-start | bytes 3145732
  101.3 54.1 %collective-permute-start.5 = (bf16[2304,512]{1,0:T(8,128)(2,1)}, bf16[2304,512]{1,0:T(8,128)(2,1)}, u32[]{:S(2)}, u32[]{:S(2)}) collective-permute-start(bf16[2304,512]{1,0:T(8,128)(2,1)} %collective-permute-done.4.p0), channel_id=1, source_target_pairs={{0,2},{1,3},{2,0},{3,1},{4,6},{5,7},{6,4},{7,5}} | collective-permute-start | bytes 7077896 | tf_op jit(solution)/shard_map/ppermute | solution.py:316
  102.9 74.7 %collective-permute-start.1 = (f32[528,512]{1,0:T(8,128)S(1)}, f32[528,512]{1,0:T(8,128)S(1)}, u32[]{:S(2)}, u32[]{:S(2)}) collective-permute-start(f32[528,512]{1,0:T(8,128)S(1)} %pad_maximum_fusion.3), channel_id=1, source_target_pairs={{0,2},{1,3},{2,0},{3,1},{4,6},{5,7},{6,4},{7,5}} | collective-permute-start | bytes 3244040 | tf_op jit(solution)/shard_map/ppermute | solution.py:316
  131.2 46.7 %copy-start.3 = (bf16[1024,512]{1,0:T(8,128)(2,1)S(1)}, bf16[1024,512]{1,0:T(8,128)(2,1)}, u32[]{:S(2)}) copy-start(bf16[1024,512]{1,0:T(8,128)(2,1)} %window_attn.2) | copy-start | bytes 3145732
  132.0 95.0 %collective-permute-start.6 = (bf16[2304,512]{1,0:T(8,128)(2,1)}, bf16[2304,512]{1,0:T(8,128)(2,1)}, u32[]{:S(2)}, u32[]{:S(2)}) collective-permute-start(bf16[2304,512]{1,0:T(8,128)(2,1)} %collective-permute-done.4.p0), channel_id=1, source_target_pairs={{0,1},{1,0},{2,3},{3,2},{4,5},{5,4},{6,7},{7,6}} | collective-permute-start | bytes 7077896 | tf_op jit(solution)/shard_map/ppermute | solution.py:313
  155.4 71.7 %collective-permute-start.7 = (bf16[2304,512]{1,0:T(8,128)(2,1)}, bf16[2304,512]{1,0:T(8,128)(2,1)}, u32[]{:S(2)}, u32[]{:S(2)}) collective-permute-start(bf16[2304,512]{1,0:T(8,128)(2,1)} %collective-permute-done.5.p1), channel_id=1, source_target_pairs={{0,1},{1,0},{2,3},{3,2},{4,5},{5,4},{6,7},{7,6}} | collective-permute-start | bytes 7077896 | tf_op jit(solution)/shard_map/ppermute | solution.py:313
  178.0 1.4 copy-start.4
  178.8 26.1 %collective-permute-start.2 = (bf16[1024,512]{1,0:T(8,128)(2,1)S(1)}, bf16[1024,512]{1,0:T(8,128)(2,1)S(1)}, u32[]{:S(2)}, u32[]{:S(2)}) collective-permute-start(bf16[1024,512]{1,0:T(8,128)(2,1)S(1)} %fusion), channel_id=1, source_target_pairs={{0,4},{4,0},{1,5},{5,1},{2,6},{6,2},{3,7},{7,3}} | collective-permute-start | bytes 3145736 | tf_op jit(solution)/shard_map/ppermute | solution.py:310
  180.2 45.3 %collective-permute-start.3 = (bf16[1024,512]{1,0:T(8,128)(2,1)S(1)}, bf16[1024,512]{1,0:T(8,128)(2,1)S(1)}, u32[]{:S(2)}, u32[]{:S(2)}) collective-permute-start(bf16[1024,512]{1,0:T(8,128)(2,1)S(1)} %fusion.1), channel_id=1, source_target_pairs={{0,4},{4,0},{1,5},{5,1},{2,6},{6,2},{3,7},{7,3}} | collective-permute-start | bytes 3145736 | tf_op jit(solution)/shard_map/ppermute | solution.py:310

commit v3 on v0

v3 whole, which is shorter than its diff:
```python
import functools

import jax
import jax.numpy as jnp
from jax import lax
from jax.experimental import pallas as pl
from jax.experimental.pallas import tpu as pltpu
from jax.sharding import PartitionSpec as P

BF = jnp.bfloat16
F32 = jnp.float32
NEG = float("-inf")
QB = 128
MESH = pl.DeviceIdType.MESH


def dot(a, b, dims=((1,), (0,))):
    return lax.dot_general(a, b, (dims, ((), ())), preferred_element_type=F32)


def span(start, size):
    return pl.ds(pl.multiple_of(start, size), size)


def pair_rhs(q_pair):
    half = lax.broadcasted_iota(jnp.int32, q_pair.shape, 0) < q_pair.shape[0] // 2
    zero = jnp.zeros_like(q_pair)
    return jnp.concatenate([jnp.where(half, q_pair, zero), jnp.where(half, zero, q_pair)], axis=1)


def unpair(o_two):
    n = o_two.shape[1] // 2
    half = lax.broadcasted_iota(jnp.int32, (o_two.shape[0], n), 0) < o_two.shape[0] // 2
    return jnp.where(half, o_two[:, :n], o_two[:, n:])


def spread(stat):
    n = stat.shape[1] // 2
    return jnp.concatenate([jnp.broadcast_to(stat[0:1, :n], (64, n)), jnp.broadcast_to(stat[0:1, n:], (64, n))], axis=0)


def layer_kernel(n_seq, scale, halo, x_hbm, gcol, grow, br, wq_hbm, wk_hbm, wv_hbm, wqg_hbm, wo_hbm, wu_hbm, wd_hbm, out_hbm,
                 x, w4, wo, wu, wd, po, pu, pd, qt, kx, vx, kg, vgt, qgt, x_send, x_half, x_in, x_in2, xg,
                 go, gm, gl, in_o, in_m, in_l, gfin, bias, gmask, score, gscore, o_mine, o_peer, out_s,
                 send_sem, recv_sem, load_sem):
    rank = lax.axis_index("sp")
    peer = 1 - lax.axis_index("tp")
    core = lax.rem(rank, 2)
    mate = rank + 1 - 2 * core
    across = lax.rem(rank + 2, n_seq)
    rows, dim = x.shape
    n_glob = gcol.shape[0]
    n_pairs = qt.shape[0] // 128
    loc = qt.shape[0]
    half = n_glob // 2
    row_start = rank * rows
    n_win = 2 * halo // 128 + 1
    hid = wu.shape[1]
    piece = hid // n_seq
    depth = loc // n_seq

    loads = {}

    def load(key, src, dst):
        loads[key] = pltpu.make_async_copy(src, dst, load_sem.at[len(loads)])
        loads[key].start()

    for c in range(4):
        at = slice(512 * c, 512 * c + 512)
        load(("x", c), x_hbm.at[at, :], x.at[at, :])
    for c, w in enumerate((wk_hbm, wv_hbm, wq_hbm, wqg_hbm)):
        load(("w", c), w, w4.at[c])
    load("wo", wo_hbm, wo)
    load("wu", wu_hbm, wu)
    load("wd", wd_hbm, wd)
    wk, wv, wq, wqg = (w4.at[c] for c in range(4))

    barrier = pltpu.get_barrier_semaphore()
    for step in range(1, n_seq):
        pl.semaphore_signal(barrier, inc=1, device_id={"sp": lax.rem(rank + step, n_seq)}, device_id_type=MESH)
    pl.semaphore_signal(barrier, inc=1, device_id={"tp": peer}, device_id_type=MESH)
    pl.semaphore_wait(barrier, n_seq)

    used = [0]

    def copy(src, dst, sp=None):
        idx = used[0]
        used[0] += 1
        return pltpu.make_async_remote_copy(
            src_ref=src, dst_ref=dst, send_sem=send_sem.at[idx], recv_sem=recv_sem.at[idx],
            device_id={"tp": peer} if sp is None else {"sp": sp}, device_id_type=MESH)

    src_quarter = {
        "o": wo_hbm.at[span(rank * depth, depth), :],
        "u": wu_hbm.at[:, span(rank * piece, piece)],
        "d": wd_hbm.at[span(rank * piece, piece), :]}
    held = {"o": po, "u": pu, "d": pd}
    over_tp = {k: copy(src_quarter[k], held[k].at[0]) for k in held}
    over_x = {k: copy(held[k].at[0], held[k].at[1], across) for k in held}
    over_d = {k: copy(held[k].at[0], held[k].at[2], mate) for k in held}
    over_d2 = {k: copy(held[k].at[1], held[k].at[3], mate) for k in held}
    for k in ("o", "u", "d"):
        over_tp[k].start()

    def relay(k):
        over_tp[k].wait()
        over_x[k].start()
        over_d[k].start()

    def relay2(k):
        over_x[k].wait()
        over_d2[k].start()

    def picked(which):
        slots = gcol[span(which * half, half), :] - row_start
        acc = None
        for c in range(rows // 512):
            at = lax.broadcasted_iota(jnp.int32, (half, 512), 1) + 512 * c
            hot = jnp.where(slots == at, 1.0, 0.0).astype(BF)
            part = dot(hot, x[512 * c:512 * c + 512, :])
            acc = part if acc is None else acc + part
        return acc.astype(BF)

    for c in range(4):
        loads["x", c].wait()
    x_send[...] = picked(1 - core)
    first = copy(x_send, x_in, mate)
    x_half[...] = picked(core)
    first.start()

    def keys(c):
        kx[span(halo + c * 256, 256), :] = dot(x[span(c * 256, 256), :], wk[...]).astype(BF)

    def values(c):
        vx[:, span(halo + c * 256, 256)] = dot(wv[...], x[span(c * 256, 256), :], ((0,), (1,))).astype(BF)

    def queries(c):
        qt[:, span(c * 256, 256)] = dot(wq[...], x[span(c * 256, 256), :], ((0,), (1,))).astype(BF) * BF(scale)

    n_blk = rows // 256
    for c in range(4):
        loads["w", c].wait()
    keys(0)
    keys(n_blk - 1)
    first.wait()
    x_half[...] = x_half[...] + x_in[...]
    values(0)
    second = copy(x_half, x_in2, across)
    second.start()
    values(n_blk - 1)
    to_right = [
        copy(kx.at[pl.ds(rows, halo), :], kx.at[pl.ds(0, halo), :], rank + 1),
        copy(vx.at[:, pl.ds(rows, halo)], vx.at[:, pl.ds(0, halo)], rank + 1)]
    to_left = [
        copy(kx.at[pl.ds(halo, halo), :], kx.at[pl.ds(halo + rows, halo), :], rank - 1),
        copy(vx.at[:, pl.ds(halo, halo)], vx.at[:, pl.ds(halo + rows, halo)], rank - 1)]

    def later(c, carry):
        keys(c)
        values(c)
        return carry

    @pl.when(rank < n_seq - 1)
    def _():
        for c in to_right:
            c.start()

    @pl.when(rank > 0)
    def _():
        for c in to_left:
            c.start()

    lax.fori_loop(1, n_blk - 1, later, 0)
    lax.fori_loop(0, n_blk, lambda c, carry: (queries(c), carry)[1], 0)

    for head in range(2 * n_pairs):
        lanes = slice((head % 2) * QB, (head % 2 + 1) * QB)
        for c in range(n_win):
            hi = 128 * (n_win - c)
            g = jnp.concatenate([br[head:head + 1, hi:hi + 128], br[head:head + 1, hi - 128:hi]], axis=1)
            rolled = pltpu.roll(jnp.broadcast_to(g, (128, 256)), 0, 1, stride=1, stride_axis=0)
            bias[head // 2, c, :, lanes] = rolled[:, :QB]
        bias[head // 2, n_win, :, lanes] = jnp.full((128, QB), NEG, F32)

    relay("o")
    second.wait()
    own = span(core * half, half)
    other = span((1 - core) * half, half)
    xg[own, :] = x_half[...] + x_in2[...]

    def project(at):
        kg[at, :] = dot(xg[at, :], wk[...]).astype(BF)
        vgt[:, at] = dot(wv[...], xg[at, :], ((0,), (1,))).astype(BF)

    def project_query(at):
        qgt[:, at] = dot(wqg[...], xg[at, :], ((0,), (1,))).astype(BF) * BF(scale)

    third = copy(xg.at[own, :], xg.at[own, :], mate)
    project_query(own)
    third.start()
    project(own)
    third.wait()
    project_query(other)
    project(other)

    n_tiles = n_glob // QB

    def glob_unit(i, carry):
        @pl.when(i == 8)
        def _():
            relay("u")
            relay2("o")

        p, t = i // n_tiles, lax.rem(i, n_tiles)
        feat = span(p * 128, 128)
        rhs = pair_rhs(qgt[feat, span(t * QB, QB)])
        top = None
        for c in range(rows // 256):
            s = dot(kx[halo + 256 * c:halo + 256 * c + 256, feat], rhs)
            gscore[256 * c:256 * c + 256, :] = s
            part = jnp.max(s.reshape(32, 8, 2 * QB), axis=0)
            top = part if top is None else jnp.maximum(top, part)
        top = jnp.max(top, axis=0, keepdims=True)
        total = None
        acc = None
        for c in range(rows // 256):
            e = jnp.exp(gscore[256 * c:256 * c + 256, :] - top)
            part = jnp.sum(e.reshape(32, 8, 2 * QB), axis=0)
            total = part if total is None else total + part
            o = dot(vx[feat, halo + 256 * c:halo + 256 * c + 256], e.astype(BF))
            acc = o if acc is None else acc + o
        go[feat, span(t * QB, QB)] = unpair(acc)
        stat = (span(p * 8, 8), span(t * 2 * QB, 2 * QB))
        gm[stat] = jnp.broadcast_to(top, (8, 2 * QB))
        gl[stat] = jnp.broadcast_to(jnp.sum(total, axis=0, keepdims=True), (8, 2 * QB))
        return carry

    lax.fori_loop(0, n_pairs * n_tiles, glob_unit, 0)

    o_half, s_half = loc // 2, gm.shape[0] // 2
    far_o, far_s = span((1 - core) * o_half, o_half), span((1 - core) * s_half, s_half)
    near_o, near_s = span(core * o_half, o_half), span(core * s_half, s_half)
    round1 = [copy(go.at[far_o, :], in_o.at[0], mate), copy(gm.at[far_s, :], in_m.at[0], mate), copy(gl.at[far_s, :], in_l.at[0], mate)]
    round2 = [copy(go.at[near_o, :], in_o.at[1], across), copy(gm.at[near_s, :], in_m.at[1], across), copy(gl.at[near_s, :], in_l.at[1], across)]
    round3 = copy(gfin.at[:, near_o], gfin.at[:, near_o], mate)

    def merge(k, last):
        for pp in range(n_pairs // 2):
            for t in range(n_tiles):
                lanes, at8 = slice(2 * QB * t, 2 * QB * t + 2 * QB), slice(8 * pp, 8 * pp + 8)
                stat = (span(core * s_half + 8 * pp, 8), lanes)
                top = jnp.maximum(gm[stat], in_m[k, at8, lanes])
                a, b = jnp.exp(gm[stat] - top), jnp.exp(in_m[k, at8, lanes] - top)
                tot = gl[stat] * a + in_l[k, at8, lanes] * b
                feat = span(core * o_half + 128 * pp, 128)
                cols = slice(QB * t, QB * t + QB)
                o = go[feat, cols] * spread(a) + in_o[k, 128 * pp:128 * pp + 128, cols] * spread(b)
                if last:
                    gfin[cols, feat] = jnp.transpose(o / spread(tot)).astype(BF)
                else:
                    gm[stat] = top
                    gl[stat] = tot
                    go[feat, cols] = o

    o_base = used[0]

    def o_copy(j):
        at = span(j * QB, QB)
        return pltpu.make_async_remote_copy(
            src_ref=o_mine.at[at, :], dst_ref=o_peer.at[at, :], send_sem=send_sem.at[o_base + j], recv_sem=recv_sem.at[o_base + j],
            device_id={"tp": peer}, device_id_type=MESH)

    def fix(j, carry):
        at = span(j * QB, QB)
        ids = row_start + j * QB + lax.broadcasted_iota(jnp.int32, (QB, n_glob), 0)
        hot = jnp.where(grow[...] == ids, 1.0, 0.0)
        is_glob = jnp.max(hot, axis=1, keepdims=True) > 0.0
        val = dot(hot.astype(BF), gfin[...])
        o_mine[at, :] = jnp.where(is_glob, val, o_mine[at, :].astype(F32)).astype(BF)
        o_copy(j).start()
        return carry

    for c in round1:
        c.start()

    @pl.when(rank < n_seq - 1)
    def _():
        for c in to_right:
            c.wait_send()
        for c in to_left:
            c.wait_recv()

    @pl.when(rank > 0)
    def _():
        for c in to_left:
            c.wait_send()
        for c in to_right:
            c.wait_recv()

    @pl.when(rank == 0)
    def _():
        kx[0:halo, :] = jnp.zeros((halo, loc), BF)
        vx[:, 0:halo] = jnp.zeros((loc, halo), BF)

    @pl.when(rank == n_seq - 1)
    def _():
        kx[halo + rows:, :] = jnp.zeros((halo, loc), BF)
        vx[:, halo + rows:] = jnp.zeros((loc, halo), BF)

    n_chunk = n_win + n_glob // 128
    fix_at = 10

    def window_block(j, carry):
        @pl.when(j == 1)
        def _():
            for c in round1:
                c.wait()
            merge(0, False)
            for c in round2:
                c.start()

        @pl.when(j == 4)
        def _():
            relay("d")

        @pl.when(j == fix_at - 1)
        def _():
            for c in round2:
                c.wait()
            merge(1, True)
            round3.start()

        @pl.when(j == fix_at)
        def _():
            round3.wait()
            lax.fori_loop(0, fix_at - 1, fix, 0)

        @pl.when(j == 12)
        def _():
            relay2("u")

        @pl.when(j >= fix_at)
        def _():
            fix(j - 1, 0)

        q_start = row_start + j * QB
        q_pos = q_start + lax.broadcasted_iota(jnp.int32, (n_glob, QB), 1)
        gmask[...] = jnp.where(jnp.abs(q_pos - gcol[...]) > halo, 0.0, NEG)
        slots = []
        for c in range(n_win):
            key_start = q_start - halo + 128 * c
            slots.append(jnp.where((key_start >= 0) & (key_start < rows * n_seq), c, n_win))
        for p in range(n_pairs):
            lanes = slice(128 * p, 128 * p + 128)
            buf = p % 2
            rhs = pair_rhs(qt[lanes, span(j * QB, QB)])
            top = None
            for c in range(n_chunk):
                if c < n_win:
                    ks = kx[span((j + c) * 128, 128), lanes]
                    extra = bias[p, slots[c]]
                else:
                    at = slice(128 * (c - n_win), 128 * (c - n_win) + 128)
                    ks = kg[at, lanes]
                    extra = jnp.concatenate([gmask[at, :], gmask[at, :]], axis=1)
                s = dot(ks, rhs) + extra
                score[buf, 128 * c:128 * c + 128, :] = s
                part = jnp.max(s.reshape(16, 8, 2 * QB), axis=0)
                top = part if top is None else jnp.maximum(top, part)
            top = jnp.max(top, axis=0, keepdims=True)
            total = None
            for c in range(n_chunk):
                at = slice(128 * c, 128 * c + 128)
                e = jnp.exp(score[buf, at, :] - top)
                score[buf, at, :] = e
                part = jnp.sum(e.reshape(16, 8, 2 * QB), axis=0)
                total = part if total is None else total + part
            inv = 1.0 / jnp.sum(total, axis=0, keepdims=True)
            w_len = 128 * n_win
            pw = (score[buf, :w_len, :] * inv).astype(BF)
            pg = (score[buf, w_len:, :] * inv).astype(BF)
            vt = vx[lanes, pl.ds(pl.multiple_of(j * QB, QB), w_len)]
            o_two = dot(vt, pw) + dot(vgt[lanes, :], pg)
            o_mine[span(j * QB, QB), lanes] = jnp.transpose(unpair(o_two)).astype(BF)
        return carry

    n_win_blk = rows // QB
    lax.fori_loop(0, n_win_blk, window_block, 0)
    fix(n_win_blk - 1, 0)

    relay2("d")
    for k in ("wo", "wu", "wd"):
        loads[k].wait()
    for k in held:
        over_d[k].wait()
        over_d2[k].wait()
    quarter = (rank, across, mate, lax.rem(mate + 2, n_seq))
    mb = 256

    def out_copy(i):
        at = span(i * mb, mb)
        return pltpu.make_async_copy(out_s.at[at, :], out_hbm.at[at, :], load_sem.at[len(loads) + i])

    def mlp_block(i, carry):
        o_copy(2 * i).wait_recv()
        o_copy(2 * i + 1).wait_recv()
        at = span(i * mb, mb)
        acc = x[at, :].astype(F32) + dot(o_mine[at, :], wo[...])
        for k in range(4):
            acc = acc + dot(o_peer[at, span(quarter[k] * depth, depth)], po[k])
        h = acc.astype(BF)
        acc = h.astype(F32)
        for k in range(8):
            cols = slice(piece * (k % 4), piece * (k % 4) + piece)
            up = wu[:, cols] if k < 4 else pu[k - 4]
            down = wd[cols, :] if k < 4 else pd[k - 4]
            act = jax.nn.gelu(dot(h, up)).astype(BF)
            acc = acc + dot(act, down)
        out_s[at, :] = acc.astype(BF)
        out_copy(i).start()
        return carry

    lax.fori_loop(0, rows // mb, mlp_block, 0)

    def drain(j, carry):
        o_copy(j).wait_send()
        return carry

    lax.fori_loop(0, n_win_blk, drain, 0)

    def flush(i, carry):
        out_copy(i).wait()
        return carry

    lax.fori_loop(0, rows // mb, flush, 0)


def solution(mesh):
    n_seq = mesh.shape["sp"]

    def local_layer(tokens, glob_pos, rel_bias, w_query, w_key, w_value, w_query_glob, w_out, w_up, w_down):
        rows, dim = tokens.shape
        heads, n_bias = rel_bias.shape
        halo = (n_bias - 1) // 2
        loc = w_query.shape[1]
        n_glob = glob_pos.shape[0]
        n_pairs = loc // 128
        n_win = 2 * halo // 128 + 1
        scale = (loc // heads) ** -0.5
        hid = w_up.shape[1]
        n_ext = rows + 2 * halo
        half = n_glob // 2
        br = jnp.pad(rel_bias[:, ::-1], ((0, 0), (128, 127)), constant_values=NEG)
        vm = pl.BlockSpec(memory_space=pltpu.VMEM)
        hbm = pl.BlockSpec(memory_space=pl.ANY)

        def buf(*shape, dtype=BF):
            return pltpu.VMEM(shape, dtype)

        return pl.pallas_call(
            functools.partial(layer_kernel, n_seq, scale, halo),
            name="layer",
            in_specs=[hbm, vm, vm, vm] + [hbm] * 7,
            out_specs=hbm,
            out_shape=jax.ShapeDtypeStruct((rows, dim), BF),
            scratch_shapes=[
                buf(rows, dim), buf(4, dim, loc), buf(loc, dim), buf(dim, hid), buf(hid, dim),
                buf(4, loc // n_seq, dim), buf(4, dim, hid // n_seq), buf(4, hid // n_seq, dim),
                buf(loc, rows), buf(n_ext, loc), buf(loc, n_ext), buf(n_glob, loc), buf(loc, n_glob), buf(loc, n_glob),
                buf(half, dim), buf(half, dim), buf(half, dim), buf(half, dim), buf(n_glob, dim),
                buf(loc, n_glob, dtype=F32), buf(n_pairs * 8, 2 * n_glob, dtype=F32), buf(n_pairs * 8, 2 * n_glob, dtype=F32),
                buf(2, loc // 2, n_glob, dtype=F32), buf(2, n_pairs * 4, 2 * n_glob, dtype=F32), buf(2, n_pairs * 4, 2 * n_glob, dtype=F32),
                buf(n_glob, loc),
                buf(n_pairs, n_win + 1, 128, 2 * QB, dtype=F32), buf(n_glob, QB, dtype=F32),
                buf(2, n_win * 128 + n_glob, 2 * QB, dtype=F32), buf(rows, 2 * QB, dtype=F32),
                buf(rows, loc), buf(rows, loc), buf(rows, dim),
                pltpu.SemaphoreType.DMA((26 + rows // QB,)), pltpu.SemaphoreType.DMA((26 + rows // QB,)),
                pltpu.SemaphoreType.DMA((32,))],
            compiler_params=pltpu.CompilerParams(vmem_limit_bytes=67043328, collective_id=0, has_side_effects=True),
        )(tokens, glob_pos[:, None], glob_pos[None, :], br, w_query, w_key, w_value, w_query_glob, w_out, w_up, w_down)

    row_spec = P(("batch", "sp"), None)
    col_spec = P(None, "tp")
    head_spec = P("tp", None)
    in_specs = (row_spec, P("batch"), head_spec, col_spec, col_spec, col_spec, col_spec, head_spec, col_spec, head_spec)
    return jax.shard_map(local_layer, mesh=mesh, in_specs=in_specs, out_specs=row_spec, check_vma=False)
```

time: 1600 us -> 164 us (0.10); the launches traced: 1570 us -> 164 us
  local copies, waits for them, and re-layouts: 887 us -> 9.12 us
  waiting for transfers between devices: 387 us -> 0 us
  matrix products: 166 us -> 0 us
  Pallas kernels: 0 us -> 155 us
  other arithmetic: 89.7 us -> 0 us
  blocking collectives: 22 us -> 0 us
    gather x5 -> x0, local copies, waits for them, and re-layouts: 783 us -> none  [the longest x2 768 us: local_layer(): band_bias = jnp.take(rel_bias, jnp.clip(rel_offs, 0, 2 * window), axis=1)]
    psum x4 -> x0, waiting for transfers between devices: 387 us -> none  [the longest x1 194 us: local_layer(): attn_proj = lax.psum(attn_part, 'tp')]
    dot_general x12 -> x0, matrix products: 166 us -> none  [the longest x1 27.9 us: local_layer(): jnp.einsum('chqk,ckhd->cqhd', (win_exp / soft_sum).astype(jnp.bfloat16),...]
    pallas_call x0 -> x1, Pallas kernels: none -> 155 us  [local_layer(): pl.pallas_call(functools.partial(layer_kernel, n_seq, scale, halo), name=...]
    reduce_sum x3 -> x0, other arithmetic: 51.1 us -> none  [the longest x1 22.5 us: local_layer(): win_exp.sum(axis=-1, keepdims=True) + glob_exp.sum(axis=-1, keepdims=True)]
    scatter x2 -> x0, local copies, waits for them, and re-layouts: 51.1 us -> none  [local_layer(): heads_out = win_out.at[slot_rows].set(glob_out, mode='drop')]
  transfers between devices with their start and end apart: 6 -> 0, of which waited for: 2 -> 0; matrix products, arithmetic and copies ran while one was open for 57% -> 0% of each run, Pallas kernels for 0% -> 0%
where the time goes in v3:
time: 164 us
  Pallas kernels  155 us (95%)
  local copies, waits for them, and re-layouts  9.12 us (6%)
    pallas_call x1, Pallas kernels, local_layer(): pl.pallas_call(functools.partial(layer_kernel, n_seq, scale, halo), name=...  155 us
    unnamed x3, local copies, waits for them, and re-layouts  6.98 us

profile of v3, /device:TPU:0, one launch (start us, length us, event | category | flops | bytes accessed | tf_op | source)
XLA Modules:
  0.0 163.9 jit_solution(8232773374157277057)
XLA Ops:
  0.0 2.3 %reverse = f32[8,640]{1,0:T(8,128)S(1)} reverse(f32[8,640]{1,0:T(8,128)} %bitcast.3), dimensions={1} | reverse | bytes 40960
  2.3 0.1 slice
  2.3 0.6 pad.4.br
  2.9 1.5 copy.11.gcol
  4.5 154.8 %layer.1 = bf16[2048,1024]{1,0:T(8,128)(2,1)} custom-call(bf16[2048,1024]{1,0:T(8,128)(2,1)} %x_hbm.1, s32[512,1]{1,0:T(8,128)} %copy.11.gcol, s32[1,512]{1,0:T(1,128)} %bitcast.5, f32[8,768]{1,0:T(8,128)} %pad.4.br, bf16[1024,512]{1,0:T(8,128)(2,1)} %wq_hbm.1, bf16[1024,512]{1,0:T(8,128)(2,1)} %wk_hbm.1, bf16[1024,512]{1,0:T(8,128)(2,1)} %wv_hbm.1, ...), custom_call_target="tpu_custom_call" | custom-call | tf_op jit(solution)/shard_map/layer/pallas_call | solution.py:460
  159.3 4.6 %copy.13 = bf16[2048,1024]{1,0:T(8,128)(2,1)} copy(bf16[2048,1024]{1,0:T(8,128)(2,1)} %layer.1) | data formatting | bytes 8388608

commit v4 on v3

--- a/solution.py
+++ b/solution.py
@@ -11,6 +11,7 @@
 F32 = jnp.float32
 NEG = float("-inf")
 QB = 128
+GROUP = 2
 MESH = pl.DeviceIdType.MESH
 
 
@@ -39,9 +40,9 @@
     return jnp.concatenate([jnp.broadcast_to(stat[0:1, :n], (64, n)), jnp.broadcast_to(stat[0:1, n:], (64, n))], axis=0)
 
 
-def layer_kernel(n_seq, scale, halo, x_hbm, gcol, grow, br, wq_hbm, wk_hbm, wv_hbm, wqg_hbm, wo_hbm, wu_hbm, wd_hbm, out_hbm,
+def layer_kernel(n_seq, scale, halo, x_hbm, grow, rel, wq_hbm, wk_hbm, wv_hbm, wqg_hbm, wo_hbm, wu_hbm, wd_hbm, out_hbm,
                  x, w4, wo, wu, wd, po, pu, pd, qt, kx, vx, kg, vgt, qgt, x_send, x_half, x_in, x_in2, xg,
-                 go, gm, gl, in_o, in_m, in_l, gfin, bias, gmask, score, gscore, o_mine, o_peer, out_s,
+                 go, gm, gl, in_o, in_m, in_l, gfin, bias, gcol, score, prob, stat_w, gscore, stat_g, o_mine, o_peer, out_s,
                  send_sem, recv_sem, load_sem):
     rank = lax.axis_index("sp")
     peer = 1 - lax.axis_index("tp")
@@ -49,7 +50,7 @@
     mate = rank + 1 - 2 * core
     across = lax.rem(rank + 2, n_seq)
     rows, dim = x.shape
-    n_glob = gcol.shape[0]
+    n_glob = grow.shape[1]
     n_pairs = qt.shape[0] // 128
     loc = qt.shape[0]
     half = n_glob // 2
@@ -90,16 +91,24 @@
             src_ref=src, dst_ref=dst, send_sem=send_sem.at[idx], recv_sem=recv_sem.at[idx],
             device_id={"tp": peer} if sp is None else {"sp": sp}, device_id_type=MESH)
 
+    hp = piece // 2
     src_quarter = {
         "o": wo_hbm.at[span(rank * depth, depth), :],
-        "u": wu_hbm.at[:, span(rank * piece, piece)],
-        "d": wd_hbm.at[span(rank * piece, piece), :]}
-    held = {"o": po, "u": pu, "d": pd}
-    over_tp = {k: copy(src_quarter[k], held[k].at[0]) for k in held}
-    over_x = {k: copy(held[k].at[0], held[k].at[1], across) for k in held}
-    over_d = {k: copy(held[k].at[0], held[k].at[2], mate) for k in held}
-    over_d2 = {k: copy(held[k].at[1], held[k].at[3], mate) for k in held}
-    for k in ("o", "u", "d"):
+        "u0": wu_hbm.at[:, span(rank * piece, hp)], "u1": wu_hbm.at[:, pl.ds(pl.multiple_of(rank * piece + hp, hp), hp)],
+        "d0": wd_hbm.at[span(rank * piece, hp), :], "d1": wd_hbm.at[pl.ds(pl.multiple_of(rank * piece + hp, hp), hp), :]}
+
+    def held(k, slot):
+        if k == "o":
+            return po.at[slot]
+        at = slice(hp * int(k[1]), hp * int(k[1]) + hp)
+        return pu.at[slot, :, at] if k[0] == "u" else pd.at[slot, at, :]
+
+    parts = tuple(src_quarter)
+    over_tp = {k: copy(src_quarter[k], held(k, 0)) for k in parts}
+    over_x = {k: copy(held(k, 0), held(k, 1), across) for k in parts}
+    over_d = {k: copy(held(k, 0), held(k, 2), mate) for k in parts}
+    over_d2 = {k: copy(held(k, 1), held(k, 3), mate) for k in parts}
+    for k in parts:
         over_tp[k].start()
 
     def relay(k):
@@ -111,8 +120,12 @@
         over_x[k].wait()
         over_d2[k].start()
 
+    for c in range(n_glob // 128):
+        at = slice(128 * c, 128 * c + 128)
+        gcol[at, :] = jnp.transpose(jnp.broadcast_to(grow[:, at].astype(F32), (128, 128)))
+
     def picked(which):
-        slots = gcol[span(which * half, half), :] - row_start
+        slots = gcol[span(which * half, half), 0:1].astype(jnp.int32) - row_start
         acc = None
         for c in range(rows // 512):
             at = lax.broadcasted_iota(jnp.int32, (half, 512), 1) + 512 * c
@@ -175,15 +188,22 @@
 
     for head in range(2 * n_pairs):
         lanes = slice((head % 2) * QB, (head % 2 + 1) * QB)
+        known = []
         for c in range(n_win):
-            hi = 128 * (n_win - c)
-            g = jnp.concatenate([br[head:head + 1, hi:hi + 128], br[head:head + 1, hi - 128:hi]], axis=1)
-            rolled = pltpu.roll(jnp.broadcast_to(g, (128, 256)), 0, 1, stride=1, stride_axis=0)
-            bias[head // 2, c, :, lanes] = rolled[:, :QB]
+            row = rel[head:head + 1, 128 * c:min(128 * c + 128, 2 * halo + 1)]
+            if row.shape[1] < 128:
+                at = lax.broadcasted_iota(jnp.int32, (1, 128), 1) + 128 * c
+                row = jnp.where(at <= 2 * halo, jnp.broadcast_to(row[:, 0:1], (1, 128)), NEG)
+            known.append(row)
+        for c in range(n_win):
+            before = known[c - 1] if c else jnp.full((1, 128), NEG, F32)
+            both = jnp.broadcast_to(jnp.concatenate([known[c], before], axis=1), (128, 256))
+            bias[head // 2, c, :, lanes] = jnp.transpose(pltpu.roll(both, 0, 1, stride=1, stride_axis=0)[:, :QB])
         bias[head // 2, n_win, :, lanes] = jnp.full((128, QB), NEG, F32)
 
+    second.wait()
     relay("o")
-    second.wait()
+    relay("u0")
     own = span(core * half, half)
     other = span((1 - core) * half, half)
     xg[own, :] = x_half[...] + x_in2[...]
@@ -205,37 +225,47 @@
 
     n_tiles = n_glob // QB
 
+    gscore[...] = jnp.zeros(gscore.shape, F32)
+    stat_g[...] = jnp.zeros(stat_g.shape, F32)
+    n_units = n_pairs * n_tiles
+
     def glob_unit(i, carry):
-        @pl.when(i == 8)
-        def _():
-            relay("u")
+        @pl.when(i == 5)
+        def _():
+            relay("u1")
+
+        @pl.when(i == 12)
+        def _():
+            relay("d0")
             relay2("o")
 
-        p, t = i // n_tiles, lax.rem(i, n_tiles)
+        new, old = jnp.minimum(i, n_units - 1), jnp.maximum(i - 1, 0)
+        p, t = new // n_tiles, lax.rem(new, n_tiles)
         feat = span(p * 128, 128)
+        p_old, t_old = old // n_tiles, lax.rem(old, n_tiles)
+        feat_old = span(p_old * 128, 128)
         rhs = pair_rhs(qgt[feat, span(t * QB, QB)])
-        top = None
+        old_top = stat_g[...]
+        top, total, acc = None, None, None
         for c in range(rows // 256):
+            at = slice(256 * c, 256 * c + 256)
+            e = jnp.exp(gscore[at, :].reshape(32, 8, 2 * QB) - old_top)
+            part = jnp.sum(e, axis=0)
+            total = part if total is None else total + part
+            o = dot(vx[feat_old, halo + 256 * c:halo + 256 * c + 256], e.reshape(256, 2 * QB).astype(BF))
+            acc = o if acc is None else acc + o
             s = dot(kx[halo + 256 * c:halo + 256 * c + 256, feat], rhs)
-            gscore[256 * c:256 * c + 256, :] = s
+            gscore[at, :] = s
             part = jnp.max(s.reshape(32, 8, 2 * QB), axis=0)
             top = part if top is None else jnp.maximum(top, part)
-        top = jnp.max(top, axis=0, keepdims=True)
-        total = None
-        acc = None
-        for c in range(rows // 256):
-            e = jnp.exp(gscore[256 * c:256 * c + 256, :] - top)
-            part = jnp.sum(e.reshape(32, 8, 2 * QB), axis=0)
-            total = part if total is None else total + part
-            o = dot(vx[feat, halo + 256 * c:halo + 256 * c + 256], e.astype(BF))
-            acc = o if acc is None else acc + o
-        go[feat, span(t * QB, QB)] = unpair(acc)
-        stat = (span(p * 8, 8), span(t * 2 * QB, 2 * QB))
-        gm[stat] = jnp.broadcast_to(top, (8, 2 * QB))
+        go[feat_old, span(t_old * QB, QB)] = unpair(acc)
+        stat = (span(p_old * 8, 8), span(t_old * 2 * QB, 2 * QB))
+        gm[stat] = old_top
         gl[stat] = jnp.broadcast_to(jnp.sum(total, axis=0, keepdims=True), (8, 2 * QB))
-        return carry
-
-    lax.fori_loop(0, n_pairs * n_tiles, glob_unit, 0)
+        stat_g[...] = jnp.broadcast_to(jnp.max(top, axis=0, keepdims=True), (8, 2 * QB))
+        return carry
+
+    lax.fori_loop(0, n_units + 1, glob_unit, 0)
 
     o_half, s_half = loc // 2, gm.shape[0] // 2
     far_o, far_s = span((1 - core) * o_half, o_half), span((1 - core) * s_half, s_half)
@@ -308,10 +338,16 @@
         vx[:, halo + rows:] = jnp.zeros((loc, halo), BF)
 
     n_chunk = n_win + n_glob // 128
-    fix_at = 10
-
-    def window_block(j, carry):
-        @pl.when(j == 1)
+    n_win_blk = rows // QB
+    per = n_pairs // GROUP
+    n_groups = n_win_blk * per
+    fix_at = 22
+    score[...] = jnp.zeros(score.shape, F32)
+    prob[...] = jnp.zeros(prob.shape, F32)
+    stat_w[...] = jnp.ones(stat_w.shape, F32)
+
+    def window_group(n, carry):
+        @pl.when(n == 2)
         def _():
             for c in round1:
                 c.wait()
@@ -319,81 +355,89 @@
             for c in round2:
                 c.start()
 
-        @pl.when(j == 4)
-        def _():
-            relay("d")
-
-        @pl.when(j == fix_at - 1)
+        @pl.when(n == 18)
+        def _():
+            relay("d1")
+
+        @pl.when(n == fix_at - 2)
         def _():
             for c in round2:
                 c.wait()
             merge(1, True)
             round3.start()
 
-        @pl.when(j == fix_at)
+        @pl.when(n == fix_at)
         def _():
             round3.wait()
-            lax.fori_loop(0, fix_at - 1, fix, 0)
-
-        @pl.when(j == 12)
-        def _():
-            relay2("u")
-
-        @pl.when(j >= fix_at)
-        def _():
-            fix(j - 1, 0)
-
+            lax.fori_loop(0, fix_at // per - 1, fix, 0)
+
+        @pl.when(n == 26)
+        def _():
+            relay2("u0")
+
+        @pl.when(n == 30)
+        def _():
+            relay2("u1")
+
+        @pl.when((n > fix_at) & (lax.rem(n, per) == 0))
+        def _():
+            fix(n // per - 2, 0)
+
+        new, old = jnp.minimum(n, n_groups - 1), jnp.maximum(n - 2, 0)
+        j, j_old = new // per, old // per
         q_start = row_start + j * QB
-        q_pos = q_start + lax.broadcasted_iota(jnp.int32, (n_glob, QB), 1)
-        gmask[...] = jnp.where(jnp.abs(q_pos - gcol[...]) > halo, 0.0, NEG)
+        q_pos = (q_start + lax.broadcasted_iota(jnp.int32, (128, QB), 1)).astype(F32)
         slots = []
         for c in range(n_win):
             key_start = q_start - halo + 128 * c
             slots.append(jnp.where((key_start >= 0) & (key_start < rows * n_seq), c, n_win))
-        for p in range(n_pairs):
-            lanes = slice(128 * p, 128 * p + 128)
-            buf = p % 2
-            rhs = pair_rhs(qt[lanes, span(j * QB, QB)])
-            top = None
-            for c in range(n_chunk):
-                if c < n_win:
-                    ks = kx[span((j + c) * 128, 128), lanes]
-                    extra = bias[p, slots[c]]
-                else:
-                    at = slice(128 * (c - n_win), 128 * (c - n_win) + 128)
-                    ks = kg[at, lanes]
-                    extra = jnp.concatenate([gmask[at, :], gmask[at, :]], axis=1)
-                s = dot(ks, rhs) + extra
-                score[buf, 128 * c:128 * c + 128, :] = s
-                part = jnp.max(s.reshape(16, 8, 2 * QB), axis=0)
-                top = part if top is None else jnp.maximum(top, part)
-            top = jnp.max(top, axis=0, keepdims=True)
-            total = None
-            for c in range(n_chunk):
-                at = slice(128 * c, 128 * c + 128)
-                e = jnp.exp(score[buf, at, :] - top)
-                score[buf, at, :] = e
-                part = jnp.sum(e.reshape(16, 8, 2 * QB), axis=0)
+        for u in range(GROUP):
+            p = lax.rem(new, per) * GROUP + u
+            feat = span(p * 128, 128)
+            feat_old = span((lax.rem(old, per) * GROUP + u) * 128, 128)
+            rhs = pair_rhs(qt[feat, span(j * QB, QB)])
+            mid_top, old_inv = stat_w[0, u], stat_w[1, u]
+            top, total, acc = None, None, None
+            for b in range(0, n_chunk, 2):
+                cs = list(range(b, min(b + 2, n_chunk)))
+                at = slice(128 * b, 128 * (cs[-1] + 1))
+                w = (prob[u, at, :].reshape(-1, 8, 2 * QB) * old_inv).reshape(-1, 2 * QB).astype(BF)
+                vs = [vx[feat_old, span((j_old + c) * 128, 128)] if c < n_win else vgt[feat_old, 128 * (c - n_win):128 * (c - n_win) + 128]
+                      for c in cs]
+                o = dot(jnp.concatenate(vs, axis=1), w)
+                acc = o if acc is None else acc + o
+                e = jnp.exp(score[u, at, :].reshape(-1, 8, 2 * QB) - mid_top)
+                prob[u, at, :] = e.reshape(-1, 2 * QB)
+                part = jnp.sum(e, axis=0)
                 total = part if total is None else total + part
-            inv = 1.0 / jnp.sum(total, axis=0, keepdims=True)
-            w_len = 128 * n_win
-            pw = (score[buf, :w_len, :] * inv).astype(BF)
-            pg = (score[buf, w_len:, :] * inv).astype(BF)
-            vt = vx[lanes, pl.ds(pl.multiple_of(j * QB, QB), w_len)]
-            o_two = dot(vt, pw) + dot(vgt[lanes, :], pg)
-            o_mine[span(j * QB, QB), lanes] = jnp.transpose(unpair(o_two)).astype(BF)
-        return carry
-
-    n_win_blk = rows // QB
-    lax.fori_loop(0, n_win_blk, window_block, 0)
+                for c in cs:
+                    if c < n_win:
+                        ks = kx[span((j + c) * 128, 128), feat]
+                        extra = bias[p, slots[c]]
+                    else:
+                        rows_g = slice(128 * (c - n_win), 128 * (c - n_win) + 128)
+                        ks = kg[rows_g, feat]
+                        mask = jnp.where(jnp.abs(q_pos - gcol[rows_g, :]) > halo, 0.0, NEG)
+                        extra = jnp.concatenate([mask, mask], axis=1)
+                    s = dot(ks, rhs) + extra
+                    score[u, 128 * c:128 * c + 128, :] = s
+                    part = jnp.max(s.reshape(16, 8, 2 * QB), axis=0)
+                    top = part if top is None else jnp.maximum(top, part)
+            o_mine[span(j_old * QB, QB), feat_old] = jnp.transpose(unpair(acc)).astype(BF)
+            stat_w[0, u] = jnp.broadcast_to(jnp.max(top, axis=0, keepdims=True), (8, 2 * QB))
+            stat_w[1, u] = jnp.broadcast_to(1.0 / jnp.sum(total, axis=0, keepdims=True), (8, 2 * QB))
+        return carry
+
+    lax.fori_loop(0, n_groups + 2, window_group, 0)
     fix(n_win_blk - 1, 0)
 
-    relay2("d")
+    relay2("d0")
     for k in ("wo", "wu", "wd"):
         loads[k].wait()
-    for k in held:
+    for k in parts:
         over_d[k].wait()
-        over_d2[k].wait()
+        if k[0] != "d":
+            over_d2[k].wait()
     quarter = (rank, across, mate, lax.rem(mate + 2, n_seq))
     mb = 256
 
@@ -410,7 +454,13 @@
             acc = acc + dot(o_peer[at, span(quarter[k] * depth, depth)], po[k])
         h = acc.astype(BF)
         acc = h.astype(F32)
-        for k in range(8):
+        for k in (0, 1, 2, 3, 4, 6, 5, 7):
+            if k == 5:
+                @pl.when(i == 0)
+                def _():
+                    relay2("d1")
+                    over_d2["d0"].wait()
+                    over_d2["d1"].wait()
             cols = slice(piece * (k % 4), piece * (k % 4) + piece)
             up = wu[:, cols] if k < 4 else pu[k - 4]
             down = wd[cols, :] if k < 4 else pd[k - 4]
@@ -450,7 +500,6 @@
         hid = w_up.shape[1]
         n_ext = rows + 2 * halo
         half = n_glob // 2
-        br = jnp.pad(rel_bias[:, ::-1], ((0, 0), (128, 127)), constant_values=NEG)
         vm = pl.BlockSpec(memory_space=pltpu.VMEM)
         hbm = pl.BlockSpec(memory_space=pl.ANY)
 
@@ -460,7 +509,7 @@
         return pl.pallas_call(
             functools.partial(layer_kernel, n_seq, scale, halo),
             name="layer",
-            in_specs=[hbm, vm, vm, vm] + [hbm] * 7,
+            in_specs=[hbm, vm, vm] + [hbm] * 7,
             out_specs=hbm,
             out_shape=jax.ShapeDtypeStruct((rows, dim), BF),
             scratch_shapes=[
@@ -472,12 +521,13 @@
                 buf(2, loc // 2, n_glob, dtype=F32), buf(2, n_pairs * 4, 2 * n_glob, dtype=F32), buf(2, n_pairs * 4, 2 * n_glob, dtype=F32),
                 buf(n_glob, loc),
                 buf(n_pairs, n_win + 1, 128, 2 * QB, dtype=F32), buf(n_glob, QB, dtype=F32),
-                buf(2, n_win * 128 + n_glob, 2 * QB, dtype=F32), buf(rows, 2 * QB, dtype=F32),
+                buf(GROUP, n_win * 128 + n_glob, 2 * QB, dtype=F32), buf(GROUP, n_win * 128 + n_glob, 2 * QB, dtype=F32),
+                buf(2, GROUP, 8, 2 * QB, dtype=F32), buf(rows, 2 * QB, dtype=F32), buf(8, 2 * QB, dtype=F32),
                 buf(rows, loc), buf(rows, loc), buf(rows, dim),
-                pltpu.SemaphoreType.DMA((26 + rows // QB,)), pltpu.SemaphoreType.DMA((26 + rows // QB,)),
+                pltpu.SemaphoreType.DMA((34 + rows // QB,)), pltpu.SemaphoreType.DMA((34 + rows // QB,)),
                 pltpu.SemaphoreType.DMA((32,))],
             compiler_params=pltpu.CompilerParams(vmem_limit_bytes=67043328, collective_id=0, has_side_effects=True),
-        )(tokens, glob_pos[:, None], glob_pos[None, :], br, w_query, w_key, w_value, w_query_glob, w_out, w_up, w_down)
+        )(tokens, glob_pos[None, :], rel_bias, w_query, w_key, w_value, w_query_glob, w_out, w_up, w_down)
 
     row_spec = P(("batch", "sp"), None)
     col_spec = P(None, "tp")

time: 164 us -> 166 us (1.012)
  Pallas kernels: 155 us -> 161 us
  local copies, waits for them, and re-layouts: 9.12 us -> 4.64 us
    pallas_call x1, Pallas kernels: 155 us -> 161 us  [local_layer(): pl.pallas_call(functools.partial(layer_kernel, n_seq, scale, halo), name=...]
    unnamed x3 -> x1, local copies, waits for them, and re-layouts: 6.98 us -> 4.64 us
where the time goes in v4:
time: 166 us
  Pallas kernels  161 us (97%)
  local copies, waits for them, and re-layouts  4.64 us (3%)
    pallas_call x1, Pallas kernels, local_layer(): pl.pallas_call(functools.partial(layer_kernel, n_seq, scale, halo), name=...  161 us
    unnamed x1, local copies, waits for them, and re-layouts  4.64 us

profile of v4, /device:TPU:0, one launch (start us, length us, event | category | flops | bytes accessed | tf_op | source)
XLA Modules:
  0.0 166.0 jit_solution(8359852379543816847)
XLA Ops:
  0.0 161.4 %layer.1 = bf16[2048,1024]{1,0:T(8,128)(2,1)} custom-call(bf16[2048,1024]{1,0:T(8,128)(2,1)} %x_hbm.1, s32[1,512]{1,0:T(1,128)} %bitcast.1, f32[8,513]{1,0:T(8,128)} %rel.1, bf16[1024,512]{1,0:T(8,128)(2,1)} %wq_hbm.1, bf16[1024,512]{1,0:T(8,128)(2,1)} %wk_hbm.1, bf16[1024,512]{1,0:T(8,128)(2,1)} %wv_hbm.1, bf16[1024,512]{1,0:T(8,128)(2,1)} %wqg_hbm.1, ...), custom_call_target="tpu_custom_call" | custom-call | tf_op jit(solution)/shard_map/layer/pallas_call | solution.py:509
  161.4 4.6 %copy.12 = bf16[2048,1024]{1,0:T(8,128)(2,1)} copy(bf16[2048,1024]{1,0:T(8,128)(2,1)} %layer.1) | data formatting | bytes 8388608

commit v5 on v4

--- a/solution.py
+++ b/solution.py
@@ -105,15 +105,20 @@
 
     parts = tuple(src_quarter)
     over_tp = {k: copy(src_quarter[k], held(k, 0)) for k in parts}
-    over_x = {k: copy(held(k, 0), held(k, 1), across) for k in parts}
+    over_x = {k: copy(held(k, 0), held(k, 1), across) for k in parts if k != "d1"}
     over_d = {k: copy(held(k, 0), held(k, 2), mate) for k in parts}
     over_d2 = {k: copy(held(k, 1), held(k, 3), mate) for k in parts}
-    for k in parts:
+    over_x["d1"] = copy(wd_hbm.at[pl.ds(pl.multiple_of(across * piece + hp, hp), hp), :], held("d1", 1))
+    for k in ("o", "u0", "u1"):
         over_tp[k].start()
+    then = {"o": over_tp["d0"], "u0": over_tp["d1"], "u1": over_x["d1"]}
 
     def relay(k):
         over_tp[k].wait()
-        over_x[k].start()
+        if k in then:
+            then[k].start()
+        if k != "d1":
+            over_x[k].start()
         over_d[k].start()
 
     def relay2(k):
@@ -230,13 +235,8 @@
     n_units = n_pairs * n_tiles
 
     def glob_unit(i, carry):
-        @pl.when(i == 5)
-        def _():
-            relay("u1")
-
-        @pl.when(i == 12)
-        def _():
-            relay("d0")
+        @pl.when(i == 8)
+        def _():
             relay2("o")
 
         new, old = jnp.minimum(i, n_units - 1), jnp.maximum(i - 1, 0)
@@ -341,7 +341,7 @@
     n_win_blk = rows // QB
     per = n_pairs // GROUP
     n_groups = n_win_blk * per
-    fix_at = 22
+    fix_at = 20
     score[...] = jnp.zeros(score.shape, F32)
     prob[...] = jnp.zeros(prob.shape, F32)
     stat_w[...] = jnp.ones(stat_w.shape, F32)
@@ -354,10 +354,15 @@
             merge(0, False)
             for c in round2:
                 c.start()
-
-        @pl.when(n == 18)
-        def _():
-            relay("d1")
+            relay("u1")
+
+        @pl.when(n == 6)
+        def _():
+            relay2("u0")
+
+        @pl.when(n == 9)
+        def _():
+            relay("d0")
 
         @pl.when(n == fix_at - 2)
         def _():
@@ -369,15 +374,16 @@
         @pl.when(n == fix_at)
         def _():
             round3.wait()
+            relay("d1")
             lax.fori_loop(0, fix_at // per - 1, fix, 0)
 
-        @pl.when(n == 26)
-        def _():
-            relay2("u0")
+        @pl.when(n == 28)
+        def _():
+            relay2("u1")
 
         @pl.when(n == 30)
         def _():
-            relay2("u1")
+            relay2("d1")
 
         @pl.when((n > fix_at) & (lax.rem(n, per) == 0))
         def _():
@@ -391,47 +397,51 @@
         for c in range(n_win):
             key_start = q_start - halo + 128 * c
             slots.append(jnp.where((key_start >= 0) & (key_start < rows * n_seq), c, n_win))
-        for u in range(GROUP):
-            p = lax.rem(new, per) * GROUP + u
-            feat = span(p * 128, 128)
-            feat_old = span((lax.rem(old, per) * GROUP + u) * 128, 128)
-            rhs = pair_rhs(qt[feat, span(j * QB, QB)])
-            mid_top, old_inv = stat_w[0, u], stat_w[1, u]
-            top, total, acc = None, None, None
-            for b in range(0, n_chunk, 2):
-                cs = list(range(b, min(b + 2, n_chunk)))
-                at = slice(128 * b, 128 * (cs[-1] + 1))
-                w = (prob[u, at, :].reshape(-1, 8, 2 * QB) * old_inv).reshape(-1, 2 * QB).astype(BF)
-                vs = [vx[feat_old, span((j_old + c) * 128, 128)] if c < n_win else vgt[feat_old, 128 * (c - n_win):128 * (c - n_win) + 128]
+        units = range(GROUP)
+        p = [lax.rem(new, per) * GROUP + u for u in units]
+        feat = [span(p[u] * 128, 128) for u in units]
+        feat_old = [span((lax.rem(old, per) * GROUP + u) * 128, 128) for u in units]
+        rhs = [pair_rhs(qt[feat[u], span(j * QB, QB)]) for u in units]
+        mid_top, old_inv = [stat_w[0, u] for u in units], [stat_w[1, u] for u in units]
+        top, total, acc = [None] * GROUP, [None] * GROUP, [None] * GROUP
+
+        def plus(a, b):
+            return b if a is None else a + b
+
+        for b in range(0, n_chunk, 2):
+            cs = list(range(b, min(b + 2, n_chunk)))
+            at = slice(128 * b, 128 * (cs[-1] + 1))
+            for u in units:
+                w = (prob[u, at, :].reshape(-1, 8, 2 * QB) * old_inv[u]).reshape(-1, 2 * QB).astype(BF)
+                vs = [vx[feat_old[u], span((j_old + c) * 128, 128)] if c < n_win else vgt[feat_old[u], 128 * (c - n_win):128 * (c - n_win) + 128]
                       for c in cs]
-                o = dot(jnp.concatenate(vs, axis=1), w)
-                acc = o if acc is None else acc + o
-                e = jnp.exp(score[u, at, :].reshape(-1, 8, 2 * QB) - mid_top)
+                acc[u] = plus(acc[u], dot(jnp.concatenate(vs, axis=1), w))
+            for u in units:
+                e = jnp.exp(score[u, at, :].reshape(-1, 8, 2 * QB) - mid_top[u])
                 prob[u, at, :] = e.reshape(-1, 2 * QB)
-                part = jnp.sum(e, axis=0)
-                total = part if total is None else total + part
-                for c in cs:
+                total[u] = plus(total[u], jnp.sum(e, axis=0))
+            for c in cs:
+                if c >= n_win:
+                    rows_g = slice(128 * (c - n_win), 128 * (c - n_win) + 128)
+                    mask = jnp.where(jnp.abs(q_pos - gcol[rows_g, :]) > halo, 0.0, NEG)
+                    mask = jnp.concatenate([mask, mask], axis=1)
+                for u in units:
                     if c < n_win:
-                        ks = kx[span((j + c) * 128, 128), feat]
-                        extra = bias[p, slots[c]]
+                        s = dot(kx[span((j + c) * 128, 128), feat[u]], rhs[u]) + bias[p[u], slots[c]]
                     else:
-                        rows_g = slice(128 * (c - n_win), 128 * (c - n_win) + 128)
-                        ks = kg[rows_g, feat]
-                        mask = jnp.where(jnp.abs(q_pos - gcol[rows_g, :]) > halo, 0.0, NEG)
-                        extra = jnp.concatenate([mask, mask], axis=1)
-                    s = dot(ks, rhs) + extra
+                        s = dot(kg[rows_g, feat[u]], rhs[u]) + mask
                     score[u, 128 * c:128 * c + 128, :] = s
                     part = jnp.max(s.reshape(16, 8, 2 * QB), axis=0)
-                    top = part if top is None else jnp.maximum(top, part)
-            o_mine[span(j_old * QB, QB), feat_old] = jnp.transpose(unpair(acc)).astype(BF)
-            stat_w[0, u] = jnp.broadcast_to(jnp.max(top, axis=0, keepdims=True), (8, 2 * QB))
-            stat_w[1, u] = jnp.broadcast_to(1.0 / jnp.sum(total, axis=0, keepdims=True), (8, 2 * QB))
+                    top[u] = part if top[u] is None else jnp.maximum(top[u], part)
+        for u in units:
+            o_mine[span(j_old * QB, QB), feat_old[u]] = jnp.transpose(unpair(acc[u])).astype(BF)
+            stat_w[0, u] = jnp.broadcast_to(jnp.max(top[u], axis=0, keepdims=True), (8, 2 * QB))
+            stat_w[1, u] = jnp.broadcast_to(1.0 / jnp.sum(total[u], axis=0, keepdims=True), (8, 2 * QB))
         return carry
 
     lax.fori_loop(0, n_groups + 2, window_group, 0)
     fix(n_win_blk - 1, 0)
 
-    relay2("d0")
     for k in ("wo", "wu", "wd"):
         loads[k].wait()
     for k in parts:
@@ -458,7 +468,7 @@
             if k == 5:
                 @pl.when(i == 0)
                 def _():
-                    relay2("d1")
+                    relay2("d0")
                     over_d2["d0"].wait()
                     over_d2["d1"].wait()
             cols = slice(piece * (k % 4), piece * (k % 4) + piece)

time: 166 us -> 144 us (0.87)
  Pallas kernels: 161 us -> 139 us
    pallas_call x1, Pallas kernels: 161 us -> 139 us  [local_layer(): pl.pallas_call(functools.partial(layer_kernel, n_seq, scale, halo), name=...]
where the time goes in v5:
time: 144 us
  Pallas kernels  139 us (97%)
  local copies, waits for them, and re-layouts  4.64 us (3%)
    pallas_call x1, Pallas kernels, local_layer(): pl.pallas_call(functools.partial(layer_kernel, n_seq, scale, halo), name=...  139 us
    unnamed x1, local copies, waits for them, and re-layouts  4.64 us

profile of v5, /device:TPU:0, one launch (start us, length us, event | category | flops | bytes accessed | tf_op | source)
XLA Modules:
  0.0 143.6 jit_solution(4087908779672510952)
XLA Ops:
  0.0 138.9 %layer.1 = bf16[2048,1024]{1,0:T(8,128)(2,1)} custom-call(bf16[2048,1024]{1,0:T(8,128)(2,1)} %x_hbm.1, s32[1,512]{1,0:T(1,128)} %bitcast.1, f32[8,513]{1,0:T(8,128)} %rel.1, bf16[1024,512]{1,0:T(8,128)(2,1)} %wq_hbm.1, bf16[1024,512]{1,0:T(8,128)(2,1)} %wk_hbm.1, bf16[1024,512]{1,0:T(8,128)(2,1)} %wv_hbm.1, bf16[1024,512]{1,0:T(8,128)(2,1)} %wqg_hbm.1, ...), custom_call_target="tpu_custom_call" | custom-call | tf_op jit(solution)/shard_map/layer/pallas_call | solution.py:519
  138.9 4.6 %copy.12 = bf16[2048,1024]{1,0:T(8,128)(2,1)} copy(bf16[2048,1024]{1,0:T(8,128)(2,1)} %layer.1) | data formatting | bytes 8388608

commit v6 on v5

--- a/solution.py
+++ b/solution.py
@@ -40,9 +40,9 @@
     return jnp.concatenate([jnp.broadcast_to(stat[0:1, :n], (64, n)), jnp.broadcast_to(stat[0:1, n:], (64, n))], axis=0)
 
 
-def layer_kernel(n_seq, scale, halo, x_hbm, grow, rel, wq_hbm, wk_hbm, wv_hbm, wqg_hbm, wo_hbm, wu_hbm, wd_hbm, out_hbm,
+def layer_kernel(n_seq, scale, halo, x_hbm, grow, rel, wq_hbm, wk_hbm, wv_hbm, wqg_hbm, wo_hbm, wu_hbm, wd_hbm, out_ref,
                  x, w4, wo, wu, wd, po, pu, pd, qt, kx, vx, kg, vgt, qgt, x_send, x_half, x_in, x_in2, xg,
-                 go, gm, gl, in_o, in_m, in_l, gfin, bias, gcol, score, prob, stat_w, gscore, stat_g, o_mine, o_peer, out_s,
+                 go, gm, gl, in_o, in_m, in_l, gfin, bias, gcol, score, prob, stat_w, gscore, stat_g, o_mine, o_peer,
                  send_sem, recv_sem, load_sem):
     rank = lax.axis_index("sp")
     peer = 1 - lax.axis_index("tp")
@@ -64,7 +64,6 @@
 
     def load(key, src, dst):
         loads[key] = pltpu.make_async_copy(src, dst, load_sem.at[len(loads)])
-        loads[key].start()
 
     for c in range(4):
         at = slice(512 * c, 512 * c + 512)
@@ -74,6 +73,10 @@
     load("wo", wo_hbm, wo)
     load("wu", wu_hbm, wu)
     load("wd", wd_hbm, wd)
+    for c in range(4):
+        loads["x", c].start()
+    for c in range(2):
+        loads["w", c].start()
     wk, wv, wq, wqg = (w4.at[c] for c in range(4))
 
     barrier = pltpu.get_barrier_semaphore()
@@ -99,14 +102,14 @@
 
     def held(k, slot):
         if k == "o":
-            return po.at[slot]
+            return po.at[span((across if slot in (1, 3) else rank) * depth, depth), :]
         at = slice(hp * int(k[1]), hp * int(k[1]) + hp)
         return pu.at[slot, :, at] if k[0] == "u" else pd.at[slot, at, :]
 
     parts = tuple(src_quarter)
     over_tp = {k: copy(src_quarter[k], held(k, 0)) for k in parts}
-    over_x = {k: copy(held(k, 0), held(k, 1), across) for k in parts if k != "d1"}
-    over_d = {k: copy(held(k, 0), held(k, 2), mate) for k in parts}
+    over_x = {k: copy(held(k, 0), held(k, 0 if k == "o" else 1), across) for k in parts if k != "d1"}
+    over_d = {k: copy(held(k, 0), held(k, 0 if k == "o" else 2), mate) for k in parts}
     over_d2 = {k: copy(held(k, 1), held(k, 3), mate) for k in parts}
     over_x["d1"] = copy(wd_hbm.at[pl.ds(pl.multiple_of(across * piece + hp, hp), hp), :], held("d1", 1))
     for k in ("o", "u0", "u1"):
@@ -129,21 +132,23 @@
         at = slice(128 * c, 128 * c + 128)
         gcol[at, :] = jnp.transpose(jnp.broadcast_to(grow[:, at].astype(F32), (128, 128)))
 
-    def picked(which):
+    def picked(which, fresh):
         slots = gcol[span(which * half, half), 0:1].astype(jnp.int32) - row_start
         acc = None
         for c in range(rows // 512):
             at = lax.broadcasted_iota(jnp.int32, (half, 512), 1) + 512 * c
             hot = jnp.where(slots == at, 1.0, 0.0).astype(BF)
+            if fresh:
+                loads["x", c].wait()
             part = dot(hot, x[512 * c:512 * c + 512, :])
             acc = part if acc is None else acc + part
         return acc.astype(BF)
 
-    for c in range(4):
-        loads["x", c].wait()
-    x_send[...] = picked(1 - core)
+    x_send[...] = picked(1 - core, True)
+    for c in range(2, 4):
+        loads["w", c].start()
     first = copy(x_send, x_in, mate)
-    x_half[...] = picked(core)
+    x_half[...] = picked(core, False)
     first.start()
 
     def keys(c):
@@ -156,7 +161,7 @@
         qt[:, span(c * 256, 256)] = dot(wq[...], x[span(c * 256, 256), :], ((0,), (1,))).astype(BF) * BF(scale)
 
     n_blk = rows // 256
-    for c in range(4):
+    for c in range(2):
         loads["w", c].wait()
     keys(0)
     keys(n_blk - 1)
@@ -189,6 +194,10 @@
             c.start()
 
     lax.fori_loop(1, n_blk - 1, later, 0)
+    for c in range(2, 4):
+        loads["w", c].wait()
+    for k in ("wo", "wu", "wd"):
+        loads[k].start()
     lax.fori_loop(0, n_blk, lambda c, carry: (queries(c), carry)[1], 0)
 
     for head in range(2 * n_pairs):
@@ -448,20 +457,14 @@
         over_d[k].wait()
         if k[0] != "d":
             over_d2[k].wait()
-    quarter = (rank, across, mate, lax.rem(mate + 2, n_seq))
     mb = 256
-
-    def out_copy(i):
-        at = span(i * mb, mb)
-        return pltpu.make_async_copy(out_s.at[at, :], out_hbm.at[at, :], load_sem.at[len(loads) + i])
 
     def mlp_block(i, carry):
         o_copy(2 * i).wait_recv()
         o_copy(2 * i + 1).wait_recv()
         at = span(i * mb, mb)
         acc = x[at, :].astype(F32) + dot(o_mine[at, :], wo[...])
-        for k in range(4):
-            acc = acc + dot(o_peer[at, span(quarter[k] * depth, depth)], po[k])
+        acc = acc + dot(o_peer[at, :], po[...])
         h = acc.astype(BF)
         acc = h.astype(F32)
         for k in (0, 1, 2, 3, 4, 6, 5, 7):
@@ -476,8 +479,7 @@
             down = wd[cols, :] if k < 4 else pd[k - 4]
             act = jax.nn.gelu(dot(h, up)).astype(BF)
             acc = acc + dot(act, down)
-        out_s[at, :] = acc.astype(BF)
-        out_copy(i).start()
+        out_ref[at, :] = acc.astype(BF)
         return carry
 
     lax.fori_loop(0, rows // mb, mlp_block, 0)
@@ -487,12 +489,6 @@
         return carry
 
     lax.fori_loop(0, n_win_blk, drain, 0)
-
-    def flush(i, carry):
-        out_copy(i).wait()
-        return carry
-
-    lax.fori_loop(0, rows // mb, flush, 0)
 
 
 def solution(mesh):
@@ -520,11 +516,11 @@
             functools.partial(layer_kernel, n_seq, scale, halo),
             name="layer",
             in_specs=[hbm, vm, vm] + [hbm] * 7,
-            out_specs=hbm,
-            out_shape=jax.ShapeDtypeStruct((rows, dim), BF),
+            out_specs=vm,
+            out_shape=pltpu.VMEM((rows, dim), BF),
             scratch_shapes=[
                 buf(rows, dim), buf(4, dim, loc), buf(loc, dim), buf(dim, hid), buf(hid, dim),
-                buf(4, loc // n_seq, dim), buf(4, dim, hid // n_seq), buf(4, hid // n_seq, dim),
+                buf(loc, dim), buf(4, dim, hid // n_seq), buf(4, hid // n_seq, dim),
                 buf(loc, rows), buf(n_ext, loc), buf(loc, n_ext), buf(n_glob, loc), buf(loc, n_glob), buf(loc, n_glob),
                 buf(half, dim), buf(half, dim), buf(half, dim), buf(half, dim), buf(n_glob, dim),
                 buf(loc, n_glob, dtype=F32), buf(n_pairs * 8, 2 * n_glob, dtype=F32), buf(n_pairs * 8, 2 * n_glob, dtype=F32),
@@ -533,10 +529,10 @@
                 buf(n_pairs, n_win + 1, 128, 2 * QB, dtype=F32), buf(n_glob, QB, dtype=F32),
                 buf(GROUP, n_win * 128 + n_glob, 2 * QB, dtype=F32), buf(GROUP, n_win * 128 + n_glob, 2 * QB, dtype=F32),
                 buf(2, GROUP, 8, 2 * QB, dtype=F32), buf(rows, 2 * QB, dtype=F32), buf(8, 2 * QB, dtype=F32),
-                buf(rows, loc), buf(rows, loc), buf(rows, dim),
+                buf(rows, loc), buf(rows, loc),
                 pltpu.SemaphoreType.DMA((34 + rows // QB,)), pltpu.SemaphoreType.DMA((34 + rows // QB,)),
                 pltpu.SemaphoreType.DMA((32,))],
-            compiler_params=pltpu.CompilerParams(vmem_limit_bytes=67043328, collective_id=0, has_side_effects=True),
+            compiler_params=pltpu.CompilerParams(vmem_limit_bytes=62 * 10**6, collective_id=0, has_side_effects=True),
         )(tokens, glob_pos[None, :], rel_bias, w_query, w_key, w_value, w_query_glob, w_out, w_up, w_down)
 
     row_spec = P(("batch", "sp"), None)

time: 144 us -> 137 us (0.951)
  Pallas kernels: 139 us -> 135 us
  local copies, waits for them, and re-layouts: 4.64 us -> 2.02 us
    pallas_call x1, Pallas kernels: 139 us -> 135 us  [local_layer(): pl.pallas_call(functools.partial(layer_kernel, n_seq, scale, halo), name=...]
    unnamed x1, local copies, waits for them, and re-layouts: 4.64 us -> 2.02 us
where the time goes in v6:
time: 137 us
  Pallas kernels  135 us (99%)
  local copies, waits for them, and re-layouts  2.02 us (1%)
    pallas_call x1, Pallas kernels, local_layer(): pl.pallas_call(functools.partial(layer_kernel, n_seq, scale, halo), name=...  135 us

profile of v6, /device:TPU:0, one launch (start us, length us, event | category | flops | bytes accessed | tf_op | source)
XLA Modules:
  0.0 137.3 jit_solution(3182548354879633399)
XLA Ops:
  0.0 135.3 %layer.1 = bf16[2048,1024]{1,0:T(8,128)(2,1)S(1)} custom-call(bf16[2048,1024]{1,0:T(8,128)(2,1)} %x_hbm.1, s32[1,512]{1,0:T(1,128)} %bitcast.1, f32[8,513]{1,0:T(8,128)} %rel.1, bf16[1024,512]{1,0:T(8,128)(2,1)} %wq_hbm.1, bf16[1024,512]{1,0:T(8,128)(2,1)} %wk_hbm.1, bf16[1024,512]{1,0:T(8,128)(2,1)} %wv_hbm.1, bf16[1024,512]{1,0:T(8,128)(2,1)} %wqg_hbm.1, ...), custom_call_target="tpu_custom_call" | custom-call | tf_op jit(solution)/shard_map/layer/pallas_call | solution.py:515
  135.3 2.0 %copy.12 = bf16[2048,1024]{1,0:T(8,128)(2,1)} copy(bf16[2048,1024]{1,0:T(8,128)(2,1)S(1)} %layer.1) | data formatting | bytes 8388608

commit v7 on v6

--- a/solution.py
+++ b/solution.py
@@ -12,6 +12,7 @@
 NEG = float("-inf")
 QB = 128
 GROUP = 2
+LEAD = 1
 MESH = pl.DeviceIdType.MESH
 
 
@@ -261,10 +262,10 @@
             e = jnp.exp(gscore[at, :].reshape(32, 8, 2 * QB) - old_top)
             part = jnp.sum(e, axis=0)
             total = part if total is None else total + part
+            s = dot(kx[halo + 256 * c:halo + 256 * c + 256, feat], rhs)
+            gscore[at, :] = s
             o = dot(vx[feat_old, halo + 256 * c:halo + 256 * c + 256], e.reshape(256, 2 * QB).astype(BF))
             acc = o if acc is None else acc + o
-            s = dot(kx[halo + 256 * c:halo + 256 * c + 256, feat], rhs)
-            gscore[at, :] = s
             part = jnp.max(s.reshape(32, 8, 2 * QB), axis=0)
             top = part if top is None else jnp.maximum(top, part)
         go[feat_old, span(t_old * QB, QB)] = unpair(acc)
@@ -411,25 +412,34 @@
         feat = [span(p[u] * 128, 128) for u in units]
         feat_old = [span((lax.rem(old, per) * GROUP + u) * 128, 128) for u in units]
         rhs = [pair_rhs(qt[feat[u], span(j * QB, QB)]) for u in units]
-        mid_top, old_inv = [stat_w[0, u] for u in units], [stat_w[1, u] for u in units]
+        mid_top = [jnp.broadcast_to(jnp.max(stat_w[0, u], axis=0, keepdims=True), (8, 2 * QB)) for u in units]
+        old_inv = [jnp.broadcast_to(1.0 / jnp.sum(stat_w[1, u], axis=0, keepdims=True), (8, 2 * QB)) for u in units]
         top, total, acc = [None] * GROUP, [None] * GROUP, [None] * GROUP
 
         def plus(a, b):
             return b if a is None else a + b
 
-        for b in range(0, n_chunk, 2):
-            cs = list(range(b, min(b + 2, n_chunk)))
-            at = slice(128 * b, 128 * (cs[-1] + 1))
+        def chunks(b):
+            cs = list(range(2 * b, min(2 * b + 2, n_chunk)))
+            return cs, slice(128 * cs[0], 128 * (cs[-1] + 1))
+
+        def weigh(b):
+            cs, at = chunks(b)
             for u in units:
                 w = (prob[u, at, :].reshape(-1, 8, 2 * QB) * old_inv[u]).reshape(-1, 2 * QB).astype(BF)
                 vs = [vx[feat_old[u], span((j_old + c) * 128, 128)] if c < n_win else vgt[feat_old[u], 128 * (c - n_win):128 * (c - n_win) + 128]
                       for c in cs]
                 acc[u] = plus(acc[u], dot(jnp.concatenate(vs, axis=1), w))
+
+        def power(b):
+            cs, at = chunks(b)
             for u in units:
                 e = jnp.exp(score[u, at, :].reshape(-1, 8, 2 * QB) - mid_top[u])
                 prob[u, at, :] = e.reshape(-1, 2 * QB)
                 total[u] = plus(total[u], jnp.sum(e, axis=0))
-            for c in cs:
+
+        def match(b):
+            for c in chunks(b)[0]:
                 if c >= n_win:
                     rows_g = slice(128 * (c - n_win), 128 * (c - n_win) + 128)
                     mask = jnp.where(jnp.abs(q_pos - gcol[rows_g, :]) > halo, 0.0, NEG)
@@ -442,10 +452,20 @@
                     score[u, 128 * c:128 * c + 128, :] = s
                     part = jnp.max(s.reshape(16, 8, 2 * QB), axis=0)
                     top[u] = part if top[u] is None else jnp.maximum(top[u], part)
+
+        n_b = (n_chunk + 1) // 2
+        led = 0
+        for b in range(n_b):
+            for _ in range(LEAD):
+                if led < n_b:
+                    weigh(led)
+                    led += 1
+            power(b)
+            match(b)
         for u in units:
             o_mine[span(j_old * QB, QB), feat_old[u]] = jnp.transpose(unpair(acc[u])).astype(BF)
-            stat_w[0, u] = jnp.broadcast_to(jnp.max(top[u], axis=0, keepdims=True), (8, 2 * QB))
-            stat_w[1, u] = jnp.broadcast_to(1.0 / jnp.sum(total[u], axis=0, keepdims=True), (8, 2 * QB))
+            stat_w[0, u] = top[u]
+            stat_w[1, u] = total[u]
         return carry
 
     lax.fori_loop(0, n_groups + 2, window_group, 0)
@@ -467,18 +487,26 @@
         acc = acc + dot(o_peer[at, :], po[...])
         h = acc.astype(BF)
         acc = h.astype(F32)
-        for k in (0, 1, 2, 3, 4, 6, 5, 7):
+        order = (0, 1, 2, 3, 4, 6, 5, 7)
+
+        def up(k):
+            return dot(h, wu[:, piece * k:piece * k + piece] if k < 4 else pu[k - 4])
+
+        def down(k, act):
+            return dot(act, wd[piece * k:piece * k + piece, :] if k < 4 else pd[k - 4])
+
+        ahead = up(order[0])
+        for n, k in enumerate(order):
+            now = ahead
+            if n + 1 < len(order):
+                ahead = up(order[n + 1])
             if k == 5:
                 @pl.when(i == 0)
                 def _():
                     relay2("d0")
                     over_d2["d0"].wait()
                     over_d2["d1"].wait()
-            cols = slice(piece * (k % 4), piece * (k % 4) + piece)
-            up = wu[:, cols] if k < 4 else pu[k - 4]
-            down = wd[cols, :] if k < 4 else pd[k - 4]
-            act = jax.nn.gelu(dot(h, up)).astype(BF)
-            acc = acc + dot(act, down)
+            acc = acc + down(k, jax.nn.gelu(now).astype(BF))
         out_ref[at, :] = acc.astype(BF)
         return carry
 

time: 137 us -> 128 us (0.934)
  Pallas kernels: 135 us -> 126 us
    pallas_call x1, Pallas kernels: 135 us -> 126 us  [local_layer(): pl.pallas_call(functools.partial(layer_kernel, n_seq, scale, halo), name=...]
where the time goes in v7:
time: 128 us
  Pallas kernels  126 us (98%)
  local copies, waits for them, and re-layouts  2.02 us (2%)
    pallas_call x1, Pallas kernels, local_layer(): pl.pallas_call(functools.partial(layer_kernel, n_seq, scale, halo), name=...  126 us

profile of v7, /device:TPU:0, one launch (start us, length us, event | category | flops | bytes accessed | tf_op | source)
XLA Modules:
  0.0 127.9 jit_solution(6454042230164848672)
XLA Ops:
  0.0 125.9 %layer.1 = bf16[2048,1024]{1,0:T(8,128)(2,1)S(1)} custom-call(bf16[2048,1024]{1,0:T(8,128)(2,1)} %x_hbm.1, s32[1,512]{1,0:T(1,128)} %bitcast.1, f32[8,513]{1,0:T(8,128)} %rel.1, bf16[1024,512]{1,0:T(8,128)(2,1)} %wq_hbm.1, bf16[1024,512]{1,0:T(8,128)(2,1)} %wk_hbm.1, bf16[1024,512]{1,0:T(8,128)(2,1)} %wv_hbm.1, bf16[1024,512]{1,0:T(8,128)(2,1)} %wqg_hbm.1, ...), custom_call_target="tpu_custom_call" | custom-call | tf_op jit(solution)/shard_map/layer/pallas_call | solution.py:543
  125.9 2.0 %copy.12 = bf16[2048,1024]{1,0:T(8,128)(2,1)} copy(bf16[2048,1024]{1,0:T(8,128)(2,1)S(1)} %layer.1) | data formatting | bytes 8388608

commit v8 on v7

--- a/solution.py
+++ b/solution.py
@@ -98,14 +98,14 @@
     hp = piece // 2
     src_quarter = {
         "o": wo_hbm.at[span(rank * depth, depth), :],
-        "u0": wu_hbm.at[:, span(rank * piece, hp)], "u1": wu_hbm.at[:, pl.ds(pl.multiple_of(rank * piece + hp, hp), hp)],
+        "u0": wu_hbm.at[:dim // 2, span(rank * piece, piece)], "u1": wu_hbm.at[dim // 2:, span(rank * piece, piece)],
         "d0": wd_hbm.at[span(rank * piece, hp), :], "d1": wd_hbm.at[pl.ds(pl.multiple_of(rank * piece + hp, hp), hp), :]}
 
     def held(k, slot):
         if k == "o":
             return po.at[span((across if slot in (1, 3) else rank) * depth, depth), :]
-        at = slice(hp * int(k[1]), hp * int(k[1]) + hp)
-        return pu.at[slot, :, at] if k[0] == "u" else pd.at[slot, at, :]
+        size = dim // 2 if k[0] == "u" else hp
+        return (pu if k[0] == "u" else pd).at[slot, size * int(k[1]):size * int(k[1]) + size, :]
 
     parts = tuple(src_quarter)
     over_tp = {k: copy(src_quarter[k], held(k, 0)) for k in parts}
@@ -133,24 +133,31 @@
         at = slice(128 * c, 128 * c + 128)
         gcol[at, :] = jnp.transpose(jnp.broadcast_to(grow[:, at].astype(F32), (128, 128)))
 
-    def picked(which, fresh):
-        slots = gcol[span(which * half, half), 0:1].astype(jnp.int32) - row_start
+    part = half // 2
+
+    def picked(which, piece_no, fresh=False):
+        slots = gcol[span(which * half + piece_no * part, part), 0:1].astype(jnp.int32) - row_start
         acc = None
         for c in range(rows // 512):
-            at = lax.broadcasted_iota(jnp.int32, (half, 512), 1) + 512 * c
+            at = lax.broadcasted_iota(jnp.int32, (part, 512), 1) + 512 * c
             hot = jnp.where(slots == at, 1.0, 0.0).astype(BF)
             if fresh:
                 loads["x", c].wait()
-            part = dot(hot, x[512 * c:512 * c + 512, :])
-            acc = part if acc is None else acc + part
+            got = dot(hot, x[512 * c:512 * c + 512, :])
+            acc = got if acc is None else acc + got
         return acc.astype(BF)
 
-    x_send[...] = picked(1 - core, True)
+    two = [slice(0, part), slice(part, half)]
+    first = [copy(x_send.at[at, :], x_in.at[at, :], mate) for at in two]
+    second = [copy(x_half.at[at, :], x_in2.at[at, :], across) for at in two]
+    x_send[two[0], :] = picked(1 - core, 0, True)
     for c in range(2, 4):
         loads["w", c].start()
-    first = copy(x_send, x_in, mate)
-    x_half[...] = picked(core, False)
-    first.start()
+    x_send[two[1], :] = picked(1 - core, 1)
+    first[0].start()
+    x_half[two[0], :] = picked(core, 0)
+    first[1].start()
+    x_half[two[1], :] = picked(core, 1)
 
     def keys(c):
         kx[span(halo + c * 256, 256), :] = dot(x[span(c * 256, 256), :], wk[...]).astype(BF)
@@ -164,13 +171,15 @@
     n_blk = rows // 256
     for c in range(2):
         loads["w", c].wait()
+    first[0].wait()
+    x_half[two[0], :] = x_half[two[0], :] + x_in[two[0], :]
     keys(0)
+    second[0].start()
+    first[1].wait()
+    x_half[two[1], :] = x_half[two[1], :] + x_in[two[1], :]
     keys(n_blk - 1)
-    first.wait()
-    x_half[...] = x_half[...] + x_in[...]
+    second[1].start()
     values(0)
-    second = copy(x_half, x_in2, across)
-    second.start()
     values(n_blk - 1)
     to_right = [
         copy(kx.at[pl.ds(rows, halo), :], kx.at[pl.ds(0, halo), :], rank + 1),
@@ -216,12 +225,17 @@
             bias[head // 2, c, :, lanes] = jnp.transpose(pltpu.roll(both, 0, 1, stride=1, stride_axis=0)[:, :QB])
         bias[head // 2, n_win, :, lanes] = jnp.full((128, QB), NEG, F32)
 
-    second.wait()
     relay("o")
-    relay("u0")
+    second[0].wait()
     own = span(core * half, half)
     other = span((1 - core) * half, half)
-    xg[own, :] = x_half[...] + x_in2[...]
+    own_two = [span(core * half + part * c, part) for c in range(2)]
+    third = [copy(xg.at[at, :], xg.at[at, :], mate) for at in own_two]
+    xg[own_two[0], :] = x_half[two[0], :] + x_in2[two[0], :]
+    second[1].wait()
+    third[0].start()
+    xg[own_two[1], :] = x_half[two[1], :] + x_in2[two[1], :]
+    relay("u0")
 
     def project(at):
         kg[at, :] = dot(xg[at, :], wk[...]).astype(BF)
@@ -230,11 +244,11 @@
     def project_query(at):
         qgt[:, at] = dot(wqg[...], xg[at, :], ((0,), (1,))).astype(BF) * BF(scale)
 
-    third = copy(xg.at[own, :], xg.at[own, :], mate)
     project_query(own)
-    third.start()
+    third[1].start()
     project(own)
-    third.wait()
+    third[0].wait()
+    third[1].wait()
     project_query(other)
     project(other)
 
@@ -351,7 +365,7 @@
     n_win_blk = rows // QB
     per = n_pairs // GROUP
     n_groups = n_win_blk * per
-    fix_at = 20
+    fix_at = 26
     score[...] = jnp.zeros(score.shape, F32)
     prob[...] = jnp.zeros(prob.shape, F32)
     stat_w[...] = jnp.ones(stat_w.shape, F32)
@@ -384,16 +398,15 @@
         @pl.when(n == fix_at)
         def _():
             round3.wait()
+            lax.fori_loop(0, fix_at // per - 1, fix, 0)
+
+        @pl.when(n == 28)
+        def _():
+            relay2("u1")
+
+        @pl.when(n == 18)
+        def _():
             relay("d1")
-            lax.fori_loop(0, fix_at // per - 1, fix, 0)
-
-        @pl.when(n == 28)
-        def _():
-            relay2("u1")
-
-        @pl.when(n == 30)
-        def _():
-            relay2("d1")
 
         @pl.when((n > fix_at) & (lax.rem(n, per) == 0))
         def _():
@@ -470,6 +483,7 @@
 
     lax.fori_loop(0, n_groups + 2, window_group, 0)
     fix(n_win_blk - 1, 0)
+    relay2("d1")
 
     for k in ("wo", "wu", "wd"):
         loads[k].wait()
@@ -558,7 +572,7 @@
                 buf(GROUP, n_win * 128 + n_glob, 2 * QB, dtype=F32), buf(GROUP, n_win * 128 + n_glob, 2 * QB, dtype=F32),
                 buf(2, GROUP, 8, 2 * QB, dtype=F32), buf(rows, 2 * QB, dtype=F32), buf(8, 2 * QB, dtype=F32),
                 buf(rows, loc), buf(rows, loc),
-                pltpu.SemaphoreType.DMA((34 + rows // QB,)), pltpu.SemaphoreType.DMA((34 + rows // QB,)),
+                pltpu.SemaphoreType.DMA((37 + rows // QB,)), pltpu.SemaphoreType.DMA((37 + rows // QB,)),
                 pltpu.SemaphoreType.DMA((32,))],
             compiler_params=pltpu.CompilerParams(vmem_limit_bytes=62 * 10**6, collective_id=0, has_side_effects=True),
         )(tokens, glob_pos[None, :], rel_bias, w_query, w_key, w_value, w_query_glob, w_out, w_up, w_down)

time: 128 us -> 127 us (level)
  no operation moved by 1% of the time
where the time goes in v8:
time: 127 us
  Pallas kernels  125 us (98%)
  local copies, waits for them, and re-layouts  2.02 us (2%)
    pallas_call x1, Pallas kernels, local_layer(): pl.pallas_call(functools.partial(layer_kernel, n_seq, scale, halo), name=...  125 us

profile of v8, /device:TPU:0, one launch (start us, length us, event | category | flops | bytes accessed | tf_op | source)
XLA Modules:
  0.0 126.8 jit_solution(3084259255415502390)
XLA Ops:
  0.0 124.8 %layer.1 = bf16[2048,1024]{1,0:T(8,128)(2,1)S(1)} custom-call(bf16[2048,1024]{1,0:T(8,128)(2,1)} %x_hbm.1, s32[1,512]{1,0:T(1,128)} %bitcast.1, f32[8,513]{1,0:T(8,128)} %rel.1, bf16[1024,512]{1,0:T(8,128)(2,1)} %wq_hbm.1, bf16[1024,512]{1,0:T(8,128)(2,1)} %wk_hbm.1, bf16[1024,512]{1,0:T(8,128)(2,1)} %wv_hbm.1, bf16[1024,512]{1,0:T(8,128)(2,1)} %wqg_hbm.1, ...), custom_call_target="tpu_custom_call" | custom-call | tf_op jit(solution)/shard_map/layer/pallas_call | solution.py:557
  124.8 2.0 %copy.12 = bf16[2048,1024]{1,0:T(8,128)(2,1)} copy(bf16[2048,1024]{1,0:T(8,128)(2,1)S(1)} %layer.1) | data formatting | bytes 8388608

commit v9 on v8

--- a/solution.py
+++ b/solution.py
@@ -43,7 +43,7 @@
 
 def layer_kernel(n_seq, scale, halo, x_hbm, grow, rel, wq_hbm, wk_hbm, wv_hbm, wqg_hbm, wo_hbm, wu_hbm, wd_hbm, out_ref,
                  x, w4, wo, wu, wd, po, pu, pd, qt, kx, vx, kg, vgt, qgt, x_send, x_half, x_in, x_in2, xg,
-                 go, gm, gl, in_o, in_m, in_l, gfin, bias, gcol, score, prob, stat_w, gscore, stat_g, o_mine, o_peer,
+                 go, gm, gl, in_o, in_m, in_l, gfin, bias, gcol, pool, stat_w, stat_g, o_mine, o_peer,
                  send_sem, recv_sem, load_sem):
     rank = lax.axis_index("sp")
     peer = 1 - lax.axis_index("tp")
@@ -109,20 +109,14 @@
 
     parts = tuple(src_quarter)
     over_tp = {k: copy(src_quarter[k], held(k, 0)) for k in parts}
-    over_x = {k: copy(held(k, 0), held(k, 0 if k == "o" else 1), across) for k in parts if k != "d1"}
+    over_x = {k: copy(held(k, 0), held(k, 0 if k == "o" else 1), across) for k in parts}
     over_d = {k: copy(held(k, 0), held(k, 0 if k == "o" else 2), mate) for k in parts}
     over_d2 = {k: copy(held(k, 1), held(k, 3), mate) for k in parts}
-    over_x["d1"] = copy(wd_hbm.at[pl.ds(pl.multiple_of(across * piece + hp, hp), hp), :], held("d1", 1))
-    for k in ("o", "u0", "u1"):
-        over_tp[k].start()
-    then = {"o": over_tp["d0"], "u0": over_tp["d1"], "u1": over_x["d1"]}
-
-    def relay(k):
+    over_tp["o"].start()
+    over_tp["u0"].start()
+
+    def arrive(k):
         over_tp[k].wait()
-        if k in then:
-            then[k].start()
-        if k != "d1":
-            over_x[k].start()
         over_d[k].start()
 
     def relay2(k):
@@ -193,22 +187,14 @@
         values(c)
         return carry
 
-    @pl.when(rank < n_seq - 1)
-    def _():
-        for c in to_right:
-            c.start()
-
-    @pl.when(rank > 0)
-    def _():
-        for c in to_left:
-            c.start()
-
     lax.fori_loop(1, n_blk - 1, later, 0)
     for c in range(2, 4):
         loads["w", c].wait()
     for k in ("wo", "wu", "wd"):
         loads[k].start()
     lax.fori_loop(0, n_blk, lambda c, carry: (queries(c), carry)[1], 0)
+
+    over_tp["u1"].start()
 
     for head in range(2 * n_pairs):
         lanes = slice((head % 2) * QB, (head % 2 + 1) * QB)
@@ -225,7 +211,6 @@
             bias[head // 2, c, :, lanes] = jnp.transpose(pltpu.roll(both, 0, 1, stride=1, stride_axis=0)[:, :QB])
         bias[head // 2, n_win, :, lanes] = jnp.full((128, QB), NEG, F32)
 
-    relay("o")
     second[0].wait()
     own = span(core * half, half)
     other = span((1 - core) * half, half)
@@ -235,7 +220,6 @@
     second[1].wait()
     third[0].start()
     xg[own_two[1], :] = x_half[two[1], :] + x_in2[two[1], :]
-    relay("u0")
 
     def project(at):
         kg[at, :] = dot(xg[at, :], wk[...]).astype(BF)
@@ -246,6 +230,19 @@
 
     project_query(own)
     third[1].start()
+    arrive("o")
+    over_x["o"].start()
+
+    @pl.when(rank < n_seq - 1)
+    def _():
+        for c in to_right:
+            c.start()
+
+    @pl.when(rank > 0)
+    def _():
+        for c in to_left:
+            c.start()
+
     project(own)
     third[0].wait()
     third[1].wait()
@@ -254,14 +251,19 @@
 
     n_tiles = n_glob // QB
 
+    wide = n_win * 128 + n_glob
+    score = [pool.at[wide * u:wide * u + wide, :] for u in range(GROUP)]
+    prob = [pool.at[wide * (GROUP + u):wide * (GROUP + u + 1), :] for u in range(GROUP)]
+    gscore = pool.at[2 * GROUP * wide:2 * GROUP * wide + rows, :]
     gscore[...] = jnp.zeros(gscore.shape, F32)
     stat_g[...] = jnp.zeros(stat_g.shape, F32)
     n_units = n_pairs * n_tiles
 
     def glob_unit(i, carry):
-        @pl.when(i == 8)
-        def _():
-            relay2("o")
+        @pl.when(i == 3)
+        def _():
+            arrive("u0")
+            over_tp["d0"].start()
 
         new, old = jnp.minimum(i, n_units - 1), jnp.maximum(i - 1, 0)
         p, t = new // n_tiles, lax.rem(new, n_tiles)
@@ -365,9 +367,9 @@
     n_win_blk = rows // QB
     per = n_pairs // GROUP
     n_groups = n_win_blk * per
-    fix_at = 26
-    score[...] = jnp.zeros(score.shape, F32)
-    prob[...] = jnp.zeros(prob.shape, F32)
+    fix_at = 18
+    for r in score + prob:
+        r[...] = jnp.zeros(r.shape, F32)
     stat_w[...] = jnp.ones(stat_w.shape, F32)
 
     def window_group(n, carry):
@@ -378,15 +380,16 @@
             merge(0, False)
             for c in round2:
                 c.start()
-            relay("u1")
-
-        @pl.when(n == 6)
-        def _():
-            relay2("u0")
-
-        @pl.when(n == 9)
-        def _():
-            relay("d0")
+
+        @pl.when(n == 4)
+        def _():
+            arrive("u1")
+            over_tp["d1"].start()
+            relay2("o")
+
+        @pl.when(n == 30)
+        def _():
+            over_x["u1"].start()
 
         @pl.when(n == fix_at - 2)
         def _():
@@ -394,19 +397,13 @@
                 c.wait()
             merge(1, True)
             round3.start()
+            over_x["u0"].start()
+            arrive("d0")
 
         @pl.when(n == fix_at)
         def _():
             round3.wait()
             lax.fori_loop(0, fix_at // per - 1, fix, 0)
-
-        @pl.when(n == 28)
-        def _():
-            relay2("u1")
-
-        @pl.when(n == 18)
-        def _():
-            relay("d1")
 
         @pl.when((n > fix_at) & (lax.rem(n, per) == 0))
         def _():
@@ -439,7 +436,7 @@
         def weigh(b):
             cs, at = chunks(b)
             for u in units:
-                w = (prob[u, at, :].reshape(-1, 8, 2 * QB) * old_inv[u]).reshape(-1, 2 * QB).astype(BF)
+                w = (prob[u][at, :].reshape(-1, 8, 2 * QB) * old_inv[u]).reshape(-1, 2 * QB).astype(BF)
                 vs = [vx[feat_old[u], span((j_old + c) * 128, 128)] if c < n_win else vgt[feat_old[u], 128 * (c - n_win):128 * (c - n_win) + 128]
                       for c in cs]
                 acc[u] = plus(acc[u], dot(jnp.concatenate(vs, axis=1), w))
@@ -447,8 +444,8 @@
         def power(b):
             cs, at = chunks(b)
             for u in units:
-                e = jnp.exp(score[u, at, :].reshape(-1, 8, 2 * QB) - mid_top[u])
-                prob[u, at, :] = e.reshape(-1, 2 * QB)
+                e = jnp.exp(score[u][at, :].reshape(-1, 8, 2 * QB) - mid_top[u])
+                prob[u][at, :] = e.reshape(-1, 2 * QB)
                 total[u] = plus(total[u], jnp.sum(e, axis=0))
 
         def match(b):
@@ -462,7 +459,7 @@
                         s = dot(kx[span((j + c) * 128, 128), feat[u]], rhs[u]) + bias[p[u], slots[c]]
                     else:
                         s = dot(kg[rows_g, feat[u]], rhs[u]) + mask
-                    score[u, 128 * c:128 * c + 128, :] = s
+                    score[u][128 * c:128 * c + 128, :] = s
                     part = jnp.max(s.reshape(16, 8, 2 * QB), axis=0)
                     top[u] = part if top[u] is None else jnp.maximum(top[u], part)
 
@@ -483,48 +480,74 @@
 
     lax.fori_loop(0, n_groups + 2, window_group, 0)
     fix(n_win_blk - 1, 0)
-    relay2("d1")
+    relay2("u0")
+    arrive("d1")
 
     for k in ("wo", "wu", "wd"):
         loads[k].wait()
     for k in parts:
         over_d[k].wait()
-        if k[0] != "d":
-            over_d2[k].wait()
+    over_d2["o"].wait()
     mb = 256
-
-    def mlp_block(i, carry):
+    n_mb = rows // mb
+
+    def products(h, acc, order):
+        def up(k):
+            return dot(h, wu[:, piece * k:piece * k + piece] if k < 4 else pu[k - 4])
+
+        def down(k, act):
+            return dot(act, wd[piece * k:piece * k + piece, :] if k < 4 else pd[k - 4])
+
+        ahead = up(order[0])
+        for n, k in enumerate(order):
+            now = ahead
+            if n + 1 < len(order):
+                ahead = up(order[n + 1])
+            acc = acc + down(k, jax.nn.gelu(now).astype(BF))
+        return acc
+
+    def mlp_near(i, carry):
+        @pl.when(i == 1)
+        def _():
+            over_x["d0"].start()
+
+        @pl.when(i == 2)
+        def _():
+            relay2("u1")
+
+        @pl.when(i == 3)
+        def _():
+            over_x["d1"].start()
+
+        @pl.when(i == 4)
+        def _():
+            relay2("d0")
+
         o_copy(2 * i).wait_recv()
         o_copy(2 * i + 1).wait_recv()
         at = span(i * mb, mb)
         acc = x[at, :].astype(F32) + dot(o_mine[at, :], wo[...])
         acc = acc + dot(o_peer[at, :], po[...])
         h = acc.astype(BF)
-        acc = h.astype(F32)
-        order = (0, 1, 2, 3, 4, 6, 5, 7)
-
-        def up(k):
-            return dot(h, wu[:, piece * k:piece * k + piece] if k < 4 else pu[k - 4])
-
-        def down(k, act):
-            return dot(act, wd[piece * k:piece * k + piece, :] if k < 4 else pd[k - 4])
-
-        ahead = up(order[0])
-        for n, k in enumerate(order):
-            now = ahead
-            if n + 1 < len(order):
-                ahead = up(order[n + 1])
-            if k == 5:
-                @pl.when(i == 0)
-                def _():
-                    relay2("d0")
-                    over_d2["d0"].wait()
-                    over_d2["d1"].wait()
-            acc = acc + down(k, jax.nn.gelu(now).astype(BF))
-        out_ref[at, :] = acc.astype(BF)
+        x[at, :] = h
+        acc = products(h, h.astype(F32), (0, 1, 2, 3, 4, 6))
+        for c in range(dim // 256):
+            pool[span(c * rows + i * mb, mb), :] = acc[:, 256 * c:256 * c + 256]
         return carry
 
-    lax.fori_loop(0, rows // mb, mlp_block, 0)
+    def mlp_far(i, carry):
+        at = span(i * mb, mb)
+        acc = jnp.concatenate([pool[span(c * rows + i * mb, mb), :] for c in range(dim // 256)], axis=1)
+        out_ref[at, :] = products(x[at, :], acc, (5, 7)).astype(BF)
+        return carry
+
+    lax.fori_loop(0, n_mb - 2, mlp_near, 0)
+    relay2("d1")
+    for k in ("u0", "u1", "d0", "d1"):
+        over_d2[k].wait()
+    lax.fori_loop(0, n_mb - 2, mlp_far, 0)
+    lax.fori_loop(n_mb - 2, n_mb, mlp_near, 0)
+    lax.fori_loop(n_mb - 2, n_mb, mlp_far, 0)
 
     def drain(j, carry):
         o_copy(j).wait_send()
@@ -569,12 +592,11 @@
                 buf(2, loc // 2, n_glob, dtype=F32), buf(2, n_pairs * 4, 2 * n_glob, dtype=F32), buf(2, n_pairs * 4, 2 * n_glob, dtype=F32),
                 buf(n_glob, loc),
                 buf(n_pairs, n_win + 1, 128, 2 * QB, dtype=F32), buf(n_glob, QB, dtype=F32),
-                buf(GROUP, n_win * 128 + n_glob, 2 * QB, dtype=F32), buf(GROUP, n_win * 128 + n_glob, 2 * QB, dtype=F32),
-                buf(2, GROUP, 8, 2 * QB, dtype=F32), buf(rows, 2 * QB, dtype=F32), buf(8, 2 * QB, dtype=F32),
+                buf(rows * (dim // 256), 256, dtype=F32), buf(2, GROUP, 8, 2 * QB, dtype=F32), buf(8, 2 * QB, dtype=F32),
                 buf(rows, loc), buf(rows, loc),
                 pltpu.SemaphoreType.DMA((37 + rows // QB,)), pltpu.SemaphoreType.DMA((37 + rows // QB,)),
                 pltpu.SemaphoreType.DMA((32,))],
-            compiler_params=pltpu.CompilerParams(vmem_limit_bytes=62 * 10**6, collective_id=0, has_side_effects=True),
+            compiler_params=pltpu.CompilerParams(vmem_limit_bytes=627 * 10**5, collective_id=0, has_side_effects=True),
         )(tokens, glob_pos[None, :], rel_bias, w_query, w_key, w_value, w_query_glob, w_out, w_up, w_down)
 
     row_spec = P(("batch", "sp"), None)

time: 127 us -> 131 us (1.031)
  Pallas kernels: 125 us -> 128 us
    pallas_call x1, Pallas kernels: 125 us -> 128 us  [local_layer(): pl.pallas_call(functools.partial(layer_kernel, n_seq, scale, halo), name=...]
where the time goes in v9:
time: 131 us; the launch traced here: 130 us
  Pallas kernels  128 us (98%)
  local copies, waits for them, and re-layouts  2.02 us (2%)
    pallas_call x1, Pallas kernels, local_layer(): pl.pallas_call(functools.partial(layer_kernel, n_seq, scale, halo), name=...  128 us

profile of v9, /device:TPU:0, one launch (start us, length us, event | category | flops | bytes accessed | tf_op | source)
XLA Modules:
  0.0 130.5 jit_solution(12111231777097110118)
XLA Ops:
  0.0 128.4 %layer.1 = bf16[2048,1024]{1,0:T(8,128)(2,1)S(1)} custom-call(bf16[2048,1024]{1,0:T(8,128)(2,1)} %x_hbm.1, s32[1,512]{1,0:T(1,128)} %bitcast.1, f32[8,513]{1,0:T(8,128)} %rel.1, bf16[1024,512]{1,0:T(8,128)(2,1)} %wq_hbm.1, bf16[1024,512]{1,0:T(8,128)(2,1)} %wk_hbm.1, bf16[1024,512]{1,0:T(8,128)(2,1)} %wv_hbm.1, bf16[1024,512]{1,0:T(8,128)(2,1)} %wqg_hbm.1, ...), custom_call_target="tpu_custom_call" | custom-call | tf_op jit(solution)/shard_map/layer/pallas_call | solution.py:580
  128.5 2.0 %copy.12 = bf16[2048,1024]{1,0:T(8,128)(2,1)} copy(bf16[2048,1024]{1,0:T(8,128)(2,1)S(1)} %layer.1) | data formatting | bytes 8388608
